TPU v7x, 32 devices: a whole 2x2x4 slice. The times are simulated.
32 devices in a mesh: dp: 4 (over z), mx: 2 (over y), my: 4 (over x, core).
Axes of the slice: x: 2, y: 2, z: 4, core: 2. Of those that a mesh axis runs over, the one named last changes fastest.
Arguments:
- inputs: bfloat16 [768, 4096], P(('dp', 'mx', 'my')), may hold values from -6 to 6
- weight_means: bfloat16 [3, 14336, 4096], P(None, ('mx', 'my'), 'dp'), may hold values from -6 to 6
- weight_sigmas: bfloat16 [3, 14336, 4096], P(None, ('mx', 'my'), 'dp'), may hold values from 0.099609375 to 1
- weight_noise: bfloat16 [3, 14336, 4096], P(None, ('mx', 'my'), 'dp'), may hold values from -6 to 6
- input_signs: int32 [768, 4096], P(('dp', 'mx', 'my')), may hold values 0 or 1
- output_signs: int32 [2, 14336, 768], P(None, ('mx', 'my'), 'dp'), may hold values 0 or 1
- hidden_signs: int32 [14336, 768], P(('mx', 'my'), 'dp'), may hold values 0 or 1
- result_signs: int32 [768, 4096], P(('dp', 'mx', 'my')), may hold values 0 or 1
- cotangent: bfloat16 [768, 4096], P(('dp', 'mx', 'my')), may hold values from -6 to 6
Outputs:
- result: bfloat16 [768, 4096], P(('dp', 'mx', 'my'))
- input_grad: bfloat16 [768, 4096], P(('dp', 'mx', 'my'))
- mean_grad: bfloat16 [3, 14336, 4096], P(None, ('mx', 'my'), 'dp')
- sigma_grad: bfloat16 [3, 14336, 4096], P(None, ('mx', 'my'), 'dp')
All inputs are finite; a program needn't handle non-finite values. No bound on the sum of `input_signs` or of `output_signs` or of `hidden_signs` or of `result_signs` on one device may be relied on, other than what follows from the above.
Results may differ from a plain program's by a relative error of at most 0.02.
Values may be sent and summed in bfloat16 or wider, within the bound.
A program may use at most 192 MiB of HBM per device.

v0:
```python
import functools

import jax
import jax.numpy as jnp
from jax import lax
from jax.experimental import pallas as pl
from jax.experimental.pallas import tpu as pltpu
from jax.sharding import PartitionSpec as P

D = 4096
FF = 14336


def to_sign(values):
    return (2 * values - 1).astype(jnp.bfloat16)


def dot(left, right, dims):
    return lax.dot_general(left, right, (dims, ((), ())), preferred_element_type=jnp.float32)


def grad_kernel(groups, scales, pair, hid, sign, x, xf, c, cf, noise, mean, sigma):
    k = pl.program_id(0)
    rows = x.shape[0] // groups

    def emit(left, right, right_flipped, scale):
        total_mean = total_pert = None
        for g in range(groups):
            part = slice(g * rows, (g + 1) * rows)
            lg = left[part, :]
            lf = lg * sign[part, :]
            m = (scale * dot(lg, right[part, :], ((0,), (0,)))).astype(jnp.bfloat16)
            p = (scale * dot(lf, right_flipped[part, :], ((0,), (0,)))).astype(jnp.bfloat16)
            m, p = m.astype(jnp.float32), p.astype(jnp.float32)
            total_mean = m if g == 0 else total_mean + m
            total_pert = p if g == 0 else total_pert + p
        mean[...] = total_mean.astype(jnp.bfloat16)
        sigma[...] = (total_pert * noise[...].astype(jnp.float32)).astype(jnp.bfloat16)

    @pl.when(k < 2)
    def _():
        emit(pair, x, xf, scales[0])

    @pl.when(k == 2)
    def _():
        emit(hid, c, cf, scales[1])


def weight_grads(groups, scales, pair, hid, sign, x, xf, c, cf, noise):
    _, tokens, ff = pair.shape
    width = x.shape[1]
    tile = 256 if ff % 256 == 0 else ff
    whole = pl.BlockSpec((tokens, width), lambda k, i: (0, 0))
    block = pl.BlockSpec((None, tile, width), lambda k, i: (k, i, 0))
    return pl.pallas_call(
        functools.partial(grad_kernel, groups, scales),
        grid=(3, ff // tile),
        out_shape=[jax.ShapeDtypeStruct(noise.shape, jnp.bfloat16)] * 2,
        in_specs=[
            pl.BlockSpec((None, tokens, tile), lambda k, i: (jnp.minimum(k, 1), 0, i)),
            pl.BlockSpec((tokens, tile), lambda k, i: (0, i)),
            pl.BlockSpec((None, tokens, tile), lambda k, i: (k, 0, i)),
            whole,
            whole,
            whole,
            whole,
            block,
        ],
        out_specs=[block, block],
        cost_estimate=pl.CostEstimate(
            flops=12 * tokens * ff * width, bytes_accessed=18 * ff * width, transcendentals=0
        ),
    )(pair, hid, sign, x, xf, c, cf, noise)


def on_device(
    inputs,
    weight_means,
    weight_sigmas,
    weight_noise,
    input_signs,
    output_signs,
    hidden_signs,
    result_signs,
    cotangent,
):
    f32, bf16 = jnp.float32, jnp.bfloat16
    scale_in = D ** (-0.5)
    scale_out = FF ** (-0.5)
    groups = lax.axis_size("dp")

    def spread(value, signs):
        both = jnp.stack([value, to_sign(signs)])
        rows, width = value.shape
        both = lax.all_to_all(
            both.reshape(2, 1, rows, width), "dp", split_axis=3, concat_axis=1, tiled=True
        )
        both = lax.all_gather(both, ("mx", "my"), axis=2, tiled=True)
        both = both.reshape(2, -1, both.shape[3])
        return both[0], both[0] * both[1], both[1]

    x, xf, a = spread(inputs, input_signs)
    c, cf, r = spread(cotangent, result_signs)
    local_signs = jnp.concatenate([to_sign(output_signs), to_sign(hidden_signs)[None]])
    signs = lax.all_gather(jnp.swapaxes(local_signs, 1, 2), "dp", axis=1, tiled=True)
    perturb = (weight_sigmas.astype(f32) * weight_noise.astype(f32)).astype(bf16)

    def project(k, scale, left, left_flipped):
        total = scale * dot(left, weight_means[k], ((1,), (1,))) + scale * dot(
            left_flipped, perturb[k], ((1,), (1,))
        ) * signs[k].astype(f32)
        return lax.psum_scatter(
            total.astype(bf16), "dp", scatter_dimension=0, tiled=True
        ).astype(f32)

    gate = project(0, scale_in, x, xf)
    up = project(1, scale_in, x, xf)
    hid_grad = project(2, scale_out, c, cf)
    gate_sig = jax.nn.sigmoid(gate)
    hidden = (gate * gate_sig * up).astype(bf16)
    up_grad = (hid_grad * gate * gate_sig).astype(bf16)
    gate_grad = (hid_grad * up * gate_sig * (1.0 + gate * (1.0 - gate_sig))).astype(bf16)
    all_hidden = lax.all_gather(hidden, "dp", axis=0, tiled=True)
    pair = lax.all_gather(jnp.stack([gate_grad, up_grad]), "dp", axis=1, tiled=True)

    def finish(total):
        total = total.reshape(groups, -1, total.shape[1]).astype(bf16)
        total = lax.psum_scatter(total, ("mx", "my"), scatter_dimension=1, tiled=True)
        return lax.all_to_all(total, "dp", split_axis=0, concat_axis=2, tiled=True)[0]

    nat = ((1,), (0,))
    result = finish(
        scale_out * dot(all_hidden, weight_means[2], nat)
        + scale_out * dot(all_hidden * signs[2], perturb[2], nat) * r.astype(f32)
    )
    input_grad = finish(
        scale_in * (dot(pair[0], weight_means[0], nat) + dot(pair[1], weight_means[1], nat))
        + scale_in
        * (
            dot(pair[0] * signs[0], perturb[0], nat) + dot(pair[1] * signs[1], perturb[1], nat)
        )
        * a.astype(f32)
    )
    mean_grad, sigma_grad = weight_grads(
        groups, (scale_in, scale_out), pair, all_hidden, signs, x, xf, c, cf, weight_noise
    )
    return (result, input_grad, mean_grad, sigma_grad)


def solution(mesh):
    return jax.shard_map(
        on_device,
        mesh=mesh,
        in_specs=(
            P(("dp", "mx", "my"), None),
            P(None, ("mx", "my"), "dp"),
            P(None, ("mx", "my"), "dp"),
            P(None, ("mx", "my"), "dp"),
            P(("dp", "mx", "my"), None),
            P(None, ("mx", "my"), "dp"),
            P(("mx", "my"), "dp"),
            P(("dp", "mx", "my"), None),
            P(("dp", "mx", "my"), None),
        ),
        out_specs=(
            P(("dp", "mx", "my"), None),
            P(("dp", "mx", "my"), None),
            P(None, ("mx", "my"), "dp"),
            P(None, ("mx", "my"), "dp"),
        ),
        check_vma=False,
    )
```

profile of v0, /device:TPU:0, one launch (start us, length us, event | category | flops | bytes accessed | tf_op | source)
XLA Modules:
  0.0 721.5 jit_solution(15517698759662683215)
XLA Ops:
  14.8 17.8 %all_to_all.66 = bf16[4,2,24576]{2,1,0:T(2,128)(2,1)S(1)} all-to-all(bf16[4,2,24576]{2,1,0:T(2,128)(2,1)S(1)} %reshape.63), channel_id=1, replica_groups=mesh['dp'=4,'mx'=2,'my'=4] {'dp'}, dimensions={0} | all-to-all | bytes 786432 | tf_op jit(solution)/shard_map/all_to_all | solution.py:95
  48.6 13.8 %all_to_all.67 = bf16[4,2,24576]{2,1,0:T(2,128)(2,1)S(1)} all-to-all(bf16[4,2,24576]{2,1,0:T(2,128)(2,1)S(1)} %reshape.61), channel_id=1, replica_groups=mesh['dp'=4,'mx'=2,'my'=4] {'dp'}, dimensions={0} | all-to-all | bytes 786432 | tf_op jit(solution)/shard_map/all_to_all | solution.py:95
  65.4 3.3 copy.27
  68.8 15.1 %multiply_convert_fusion = bf16[3,1792,1024]{2,1,0:T(8,128)(2,1)} fusion(bf16[3,1792,1024]{2,1,0:T(8,128)(2,1)} %noise.1, bf16[3,1792,1024]{2,1,0:T(8,128)(2,1)} %param.11), kind=kLoop, calls=%fused_computation | loop fusion | flops 22020096 | bytes 33030144 | tf_op jit(solution)/shard_map/convert_element_type | solution.py:106
  83.9 3.6 fusion.59
  87.5 7.4 %fusion.14 = f32[768,1792]{1,0:T(8,128)} fusion(bf16[768,1024]{1,0:T(8,128)(2,1)S(1)} %bitcast.132, bf16[3,1792,1024]{2,1,0:T(8,128)(2,1)} %param.10), kind=kOutput, calls=%fused_computation.21 | convolution fusion | flops 2818572288 | bytes 10747904 | tf_op jit(solution)/shard_map/dot_general | solution.py:19
  94.9 124.6 %all-gather.8.cloned.1.call-done.sign = bf16[3,768,1792]{2,1,0:T(8,128)(2,1)} async-done(((bf16[3,192,1792]{2,1,0:T(8,128)(2,1)}), bf16[3,768,1792]{2,1,0:T(8,128)(2,1)}) %all-gather.8.cloned.1.call-update) | async-done | bytes 8257552 | tf_op jit(solution)/shard_map/all_gather | solution.py:105
  219.5 8.0 %fusion.3 = bf16[768,1792]{1,0:T(8,128)(2,1)} fusion(f32[768,1792]{1,0:T(8,128)} %fusion.14, bf16[768,1024]{1,0:T(8,128)(2,1)S(1)} %bitcast.142, bf16[3,1792,1024]{2,1,0:T(8,128)(2,1)} %multiply_convert_fusion, bf16[3,768,1792]{2,1,0:T(8,128)(2,1)} %all-gather.8.cloned.1.call-done.sign), kind=kOutput, calls=%fused_computation.6 | convolution fusion | flops 2826829824 | bytes 16252928 | tf_op jit(solution)/shard_map/dot_general | solution.py:19
  227.5 10.4 %reduce-scatter.12.cloned.1.call-start = ((), (), s32[]{:S(2)}) async-start(), calls=%async_computation.11 | async-start | bytes 3440640 | tf_op jit(solution)/shard_map/reduce_scatter | solution.py:112
  237.8 5.2 fusion.10
  243.0 7.1 fusion.1
  251.8 3.5 slice_multiply_fusion
  255.3 5.7 fusion.4
  261.1 6.7 add_convert_fusion
  267.9 40.4 %reduce-scatter.10.cloned.1.call-done = bf16[192,1792]{1,0:T(8,128)(2,1)} async-done(((bf16[768,1792]{1,0:T(8,128)(2,1)}), bf16[192,1792]{1,0:T(8,128)(2,1)}) %reduce-scatter.10.cloned.1.call-update) | async-done | bytes 688144 | tf_op jit(solution)/shard_map/reduce_scatter | solution.py:112
  308.3 56.7 %reduce-scatter.12.cloned.1.call-done = bf16[192,1792]{1,0:T(8,128)(2,1)} async-done(((bf16[768,1792]{1,0:T(8,128)(2,1)}), bf16[192,1792]{1,0:T(8,128)(2,1)}) %reduce-scatter.12.cloned.1.call-update) | async-done | bytes 688144 | tf_op jit(solution)/shard_map/reduce_scatter | solution.py:112
  365.0 56.1 %reduce-scatter.14.cloned.1.call-done = bf16[192,1792]{1,0:T(8,128)(2,1)} async-done(((bf16[768,1792]{1,0:T(8,128)(2,1)}), bf16[192,1792]{1,0:T(8,128)(2,1)}) %reduce-scatter.14.cloned.1.call-update) | async-done | bytes 688144 | tf_op jit(solution)/shard_map/reduce_scatter | solution.py:112
  421.1 3.5 fusion.56
  427.3 54.1 %all-gather.10.cloned.1.call-done.hid = bf16[768,1792]{1,0:T(8,128)(2,1)} async-done(((bf16[192,1792]{1,0:T(8,128)(2,1)}), bf16[768,1792]{1,0:T(8,128)(2,1)}) %all-gather.10.cloned.1.call-update) | async-done | bytes 2752528 | tf_op jit(solution)/shard_map/all_gather | solution.py:123
  481.4 6.2 fusion.18
  487.7 5.6 add_convert_fusion.2
  496.5 87.6 %all-gather.12.cloned.1.call-done.pair = bf16[2,768,1792]{2,1,0:T(8,128)(2,1)} async-done(((bf16[2,192,1792]{2,1,0:T(8,128)(2,1)}), bf16[2,768,1792]{2,1,0:T(8,128)(2,1)}) %all-gather.12.cloned.1.call-update) | async-done | bytes 5505040 | tf_op jit(solution)/shard_map/all_gather | solution.py:124
  584.1 6.2 fusion.16
  590.3 5.2 fusion.8
  595.5 6.2 fusion.17
  601.7 5.3 add_convert_fusion.1
  612.8 11.9 %reduce-scatter.16.cloned.1.call-done = bf16[24,4096]{1,0:T(8,128)(2,1)} async-done(((bf16[192,4096]{1,0:T(8,128)(2,1)}), bf16[24,4096]{1,0:T(8,128)(2,1)}) %reduce-scatter.16.cloned.1.call-update) | async-done | bytes 196624
  626.4 4.6 all-to-all-start.2
  633.7 4.6 all-to-all-done.2
  639.2 27.5 %reduce-scatter.18.cloned.1.call-done = bf16[24,4096]{1,0:T(8,128)(2,1)} async-done(((bf16[192,4096]{1,0:T(8,128)(2,1)}), bf16[24,4096]{1,0:T(8,128)(2,1)}) %reduce-scatter.18.cloned.1.call-update) | async-done | bytes 196624
  668.6 4.8 all-to-all-start.3
  673.4 39.9 %shard_map.120 = (bf16[3,1792,1024]{2,1,0:T(8,128)(2,1)}, bf16[3,1792,1024]{2,1,0:T(8,128)(2,1)}) custom-call(bf16[2,768,1792]{2,1,0:T(8,128)(2,1)} %all-gather.12.cloned.1.call-done.pair, bf16[768,1792]{1,0:T(8,128)(2,1)} %all-gather.10.cloned.1.call-done.hid, bf16[3,768,1792]{2,1,0:T(8,128)(2,1)} %all-gather.8.cloned.1.call-done.sign, ...), custom_call_target="tpu_custom_call" | custom-call | flops 16911433728 | bytes 33030144 | tf_op jit(solution)/shard_map/pallas_call | solution.py:55
  (74 shorter events, 47.9 us)
Async XLA Ops:
  7.2 76.7 %all-gather.14.cloned.1.call-start = ((), (), s32[]{:S(2)}) async-start(), calls=%async_computation.15 | async-start | bytes 3538944 | tf_op jit(solution)/shard_map/all_gather | solution.py:98
  35.6 3.4 copy-start.4
  39.0 180.5 %all-gather.8.cloned.1.call-start = ((), (), s32[]{:S(2)}) async-start(), calls=%async_computation.9 | async-start | bytes 10321920 | tf_op jit(solution)/shard_map/all_gather | solution.py:105
  41.3 1.6 copy-start.5
  41.3 1.6 copy-start.6
  42.8 209.0 %all-gather.16.cloned.1.call-start = ((), (), s32[]{:S(2)}) async-start(), calls=%async_computation.16 | async-start | bytes 3538944 | tf_op jit(solution)/shard_map/all_gather | solution.py:98
  68.7 239.6 %reduce-scatter.10.cloned.1.call-start = ((), (), s32[]{:S(2)}) async-start(), calls=%async_computation.10 | async-start | bytes 3440640 | tf_op jit(solution)/shard_map/reduce_scatter | solution.py:112
  87.5 522.6 %copy-start = (bf16[1,4,1,192,1024]{4,3,1,2,0:T(8,128)(2,1)}, bf16[1,4,1,192,1024]{4,3,1,2,0:T(8,128)(2,1)S(1)}, u32[]{:S(2)}) copy-start(bf16[1,4,1,192,1024]{4,3,1,2,0:T(8,128)(2,1)S(1)} %get-tuple-element.10) | copy-start | bytes 4718596
  227.5 137.5 %reduce-scatter.12.cloned.1.call-start = ((), (), s32[]{:S(2)}) async-start(), calls=%async_computation.11 | async-start | bytes 3440640 | tf_op jit(solution)/shard_map/reduce_scatter | solution.py:112
  250.2 171.0 %reduce-scatter.14.cloned.1.call-start = ((), (), s32[]{:S(2)}) async-start(), calls=%async_computation.13 | async-start | bytes 3440640 | tf_op jit(solution)/shard_map/reduce_scatter | solution.py:112
  251.8 9.3 %slice-start = ((s8[8257536]{0:T(1024)(128)(4,1)}), s8[4194304]{0:T(1024)(128)(4,1)S(1)}, s32[]{:S(2)}) async-start(s8[8257536]{0:T(1024)(128)(4,1)} %bitcast.155), calls=%async_computation.19 | async-start | bytes 8388608
  255.3 375.7 %copy-start.1 = (bf16[1,4,1,192,1024]{4,3,1,2,0:T(8,128)(2,1)}, bf16[1,4,1,192,1024]{4,3,1,2,0:T(8,128)(2,1)S(1)}, u32[]{:S(2)}) copy-start(bf16[1,4,1,192,1024]{4,3,1,2,0:T(8,128)(2,1)S(1)} %get-tuple-element.13) | copy-start | bytes 4718596
  255.3 5.7 slice-start.1
  267.8 213.6 %all-gather.10.cloned.1.call-start = ((), (), s32[]{:S(2)}) async-start(), calls=%async_computation.12 | async-start | bytes 3440640 | tf_op jit(solution)/shard_map/all_gather | solution.py:123
  424.7 159.4 %all-gather.12.cloned.1.call-start = ((), (), s32[]{:S(2)}) async-start(), calls=%async_computation.14 | async-start | bytes 6881280 | tf_op jit(solution)/shard_map/all_gather | solution.py:124
  427.3 197.3 %reduce-scatter.16.cloned.1.call-start = ((), (), s32[]{:S(2)}) async-start(), calls=%async_computation.17 | async-start | bytes 1769472
  481.4 6.2 copy-start.3
  481.4 6.2 copy-start.8
  496.3 170.5 %reduce-scatter.18.cloned.1.call-start = ((), (), s32[]{:S(2)}) async-start(), calls=%async_computation.18 | async-start | bytes 1769472
  584.1 6.2 copy-start.7
  595.5 6.2 copy-start.2
  626.4 11.9 %all-to-all-start.2 = ((bf16[4,24,1024]{2,1,0:T(8,128)(2,1)}), bf16[4,24,1024]{2,1,0:T(8,128)(2,1)S(1)}, u32[]{:S(2)}, u32[]{:S(2)}) async-start(bf16[4,24,1024]{2,1,0:T(8,128)(2,1)} %copy.31), calls=%async_computation.4 | async-start | bytes 393216 | tf_op jit(solution)/shard_map/all_to_all | solution.py:129
  668.6 44.7 %all-to-all-start.3 = ((bf16[4,24,1024]{2,1,0:T(8,128)(2,1)}), bf16[4,24,1024]{2,1,0:T(8,128)(2,1)S(1)}, u32[]{:S(2)}, u32[]{:S(2)}) async-start(bf16[4,24,1024]{2,1,0:T(8,128)(2,1)} %copy.33), calls=%async_computation.6 | async-start | bytes 393216 | tf_op jit(solution)/shard_map/all_to_all | solution.py:129
Sparse Core Ops, SparseCore 0:
  39.1 31.2 all-gather.13
  72.0 147.4 all-gather.7
  221.4 30.3 all-gather.15
  254.0 54.2 reduce-scatter.9
  311.0 53.9 reduce-scatter.11
  367.2 53.9 reduce-scatter.13
  424.8 56.5 all-gather.9
  483.0 101.0 all-gather.11
  588.0 36.6 reduce-scatter.15
  628.3 38.3 reduce-scatter.17
where the time goes:
time: 731 us; the launch traced here: 721 us
  waiting for transfers between devices  465 us (64%)
  matrix products  74.7 us (10%)
  Pallas kernels  39.9 us (5%)
  other arithmetic  39.6 us (5%)
  local copies, waits for them, and re-layouts  35.1 us (5%)
  blocking collectives  31.6 us (4%)
  starting transfers between devices  20.3 us (3%)
  between operations  14.9 us (2%)
    reduce_scatter x3, waiting for transfers between devices, project(): lax.psum_scatter(total.astype(bf16), 'dp', scatter_dimension=0, tiled=True)  153 us
    all_gather x1, waiting for transfers between devices, on_device(): lax.all_gather(jnp.swapaxes(local_signs, 1, 2), 'dp', axis=1, tiled=True)  125 us
    all_gather x1, waiting for transfers between devices, on_device(): lax.all_gather(jnp.stack([gate_grad, up_grad]), 'dp', axis=1, tiled=True)  87.6 us
    dot_general x12, matrix products, dot(): lax.dot_general(left, right, (dims, ((), ())), preferred_element_type=jnp...  74.7 us
    all_gather x1, waiting for transfers between devices, on_device(): all_hidden = lax.all_gather(hidden, 'dp', axis=0, tiled=True)  54.1 us
    pallas_call x1, Pallas kernels, weight_grads(): pl.pallas_call(functools.partial(grad_kernel, groups, scales), grid=(3, f...  39.9 us
    unnamed x12, waiting for transfers between devices  39.6 us
    all_to_all x2, blocking collectives, spread(): lax.all_to_all(both.reshape(2, 1, rows, width), 'dp', split_axis=3, conca...  31.6 us
  transfers between devices with their start and end apart: 12, of which 10 were waited for; matrix products, arithmetic and copies ran while one was open for 18% of the time, Pallas kernels for 6%

commit v1 on v0

v1 whole, which is shorter than its diff:
```python
import functools

import jax
import jax.numpy as jnp
from jax import lax
from jax.experimental import pallas as pl
from jax.experimental.pallas import tpu as pltpu
from jax.sharding import PartitionSpec as P

D = 4096
FF = 14336
MESH = pl.DeviceIdType.MESH
VMEM = pltpu.VMEM
DMA = pltpu.SemaphoreType.DMA


def to_sign(values):
    return (2 * values - 1).astype(jnp.bfloat16)


def dot(left, right, dims):
    return lax.dot_general(left, right, (dims, ((), ())), preferred_element_type=jnp.float32)


def remote(src, dst, send_sem, recv_sem, **where):
    return pltpu.make_async_remote_copy(
        src_ref=src, dst_ref=dst, send_sem=send_sem, recv_sem=recv_sem,
        device_id=where, device_id_type=MESH,
    )


def place():
    cores = 2 if lax.axis_size("my") % 2 == 0 else 1
    z, y, m = lax.axis_index("dp"), lax.axis_index("mx"), lax.axis_index("my")
    sizes = (lax.axis_size("dp"), lax.axis_size("mx"), lax.axis_size("my") // cores, cores)
    return (z, y, m // cores, m % cores), sizes


def greet_axes():
    (z, y, x, c), (nz, ny, nx, nc) = place()
    barrier = pltpu.get_barrier_semaphore()
    for d in range(1, nz):
        pl.semaphore_signal(barrier, inc=1, device_id={"dp": (z + d) % nz}, device_id_type=MESH)
    for d in range(1, ny):
        pl.semaphore_signal(barrier, inc=1, device_id={"mx": (y + d) % ny}, device_id_type=MESH)
    for d in range(1, nx):
        peer = ((x + d) % nx) * nc + c
        pl.semaphore_signal(barrier, inc=1, device_id={"my": peer}, device_id_type=MESH)
    for d in range(1, nc):
        peer = x * nc + (c + d) % nc
        pl.semaphore_signal(barrier, inc=1, device_id={"my": peer}, device_id_type=MESH)
    pl.semaphore_wait(barrier, nz + ny + nx + nc - 4)


class LineGather:
    def __init__(self, shard, full, s_sem, r_sem, own_sem):
        self.z, self.n = lax.axis_index("dp"), lax.axis_size("dp")
        self.shard, self.full, self.s_sem, self.r_sem = shard, full, s_sem, r_sem
        self.own = pltpu.make_async_copy(shard, full.at[self.z], own_sem)

    def copy(self, d, origin, src):
        return remote(
            src, self.full.at[origin], self.s_sem.at[d, origin], self.r_sem.at[d, origin],
            dp=(self.z + 1 - 2 * d + self.n) % self.n,
        )

    def begin(self):
        self.own.start()

        @pl.when(self.z < self.n - 1)
        def _():
            self.copy(0, self.z, self.shard).start()

        @pl.when(self.z > 0)
        def _():
            self.copy(1, self.z, self.shard).start()

    def relay(self, step):
        z, n = self.z, self.n
        for d in range(2):
            origin = z - step + 2 * d * step

            @pl.when((origin >= 0) & (origin < n))
            def _():
                copy = self.copy(d, origin, self.full.at[origin])
                copy.wait_recv()

                @pl.when((z < n - 1) if d == 0 else (z > 0))
                def _():
                    copy.start()

    def end(self):
        z, n = self.z, self.n
        self.own.wait()
        for origin in range(n):
            @pl.when((origin <= z) & (z < n - 1))
            def _():
                self.copy(0, origin, self.shard).wait_send()

            @pl.when((origin >= z) & (z > 0))
            def _():
                self.copy(1, origin, self.shard).wait_send()


def perturb_tiles(sigma, noise, out, wide, made, load, store):
    rows = made.shape[1]
    steps = out.shape[0] // rows

    def loads(i, slot):
        span = pl.ds(pl.multiple_of(i * rows, rows), rows)
        return (
            pltpu.make_async_copy(sigma.at[span], wide.at[slot, 0], load.at[slot, 0]),
            pltpu.make_async_copy(noise.at[span], wide.at[slot, 1], load.at[slot, 1]),
        )

    def stores(i, slot):
        span = pl.ds(pl.multiple_of(i * rows, rows), rows)
        return pltpu.make_async_copy(made.at[slot], out.at[span], store.at[slot])

    for copy in loads(0, 0):
        copy.start()

    def step(i, carry):
        slot = i % 2
        for copy in loads(i, slot):
            copy.wait()

        @pl.when(i + 1 < steps)
        def _():
            for copy in loads(i + 1, 1 - slot):
                copy.start()

        @pl.when(i >= 2)
        def _():
            stores(i - 2, slot).wait()

        product = wide[slot, 0].astype(jnp.float32) * wide[slot, 1].astype(jnp.float32)
        made[slot] = product.astype(made.dtype)
        stores(i, slot).start()
        return carry

    lax.fori_loop(0, steps, step, 0)
    for i in range(max(steps - 2, 0), steps):
        stores(i, i % 2).wait()


def spread_kernel(src, sigma, noise, shard, out, perturb, full, *scratch):
    z_s, z_r, a_s, a_r, b_s, b_r, c_s, c_r, own, g_s, g_r, g_own, wide, made, load, store = scratch
    (z, y, x, c), (nz, ny, nx, nc) = place()
    line = LineGather(shard, full, g_s, g_r, g_own)
    greet_axes()
    toward = 1 - 2 * ((2 * z) // nz)
    group = [(z + toward * k + nz) % nz for k in range(nz)]
    sends = []

    def start(copy):
        copy.start()
        sends.append(copy)
        return copy

    local = []
    for p in range(2):
        keep = pltpu.make_async_copy(src.at[p, :, z], out.at[p, :, z, y, x, c], own.at[p])
        keep.start()
        local.append(keep)
    for k in range(1, nz):
        for p in range(2):
            g = group[nz - k]
            start(remote(src.at[p, :, g], out.at[p, :, z, y, x, c], z_s.at[p, g], z_r.at[p, z], dp=g))

    def first(p, k):
        g = group[k]
        block = out.at[p, :, g, y, x, c]
        if k > 0:
            remote(src.at[p, :, g], block, z_s.at[p, g], z_r.at[p, g], dp=g).wait_recv()
        origin = src.at[p, :, g] if k == 0 else block
        if p == 0:
            return [
                start(remote(origin, block, a_s.at[p, g, e], a_r.at[p, g, e], my=((x + e) % nx) * nc + c))
                for e in range(1, nx)
            ]
        return [
            start(remote(origin, block, a_s.at[p, g, e], a_r.at[p, g, e], mx=(y + e) % ny))
            for e in range(1, ny)
        ]

    def second(p, k, before):
        g = group[k]
        for copy in before:
            copy.wait_recv()
        if k == 0:
            local[p].wait()
        if p == 0:
            block = out.at[p, :, g, y, :, c]
            return [
                start(remote(block, block, b_s.at[p, g, e], b_r.at[p, g, e], mx=(y + e) % ny))
                for e in range(1, ny)
            ]
        block = out.at[p, :, g, :, x, c]
        return [
            start(remote(block, block, b_s.at[p, g, e], b_r.at[p, g, e], my=((x + e) % nx) * nc + c))
            for e in range(1, nx)
        ]

    def third(p, k, before):
        g = group[k]
        for copy in before:
            copy.wait_recv()
        block = out.at[p, :, g, :, :, c]
        return [
            start(remote(block, block, c_s.at[p, g, e], c_r.at[p, g, e], my=x * nc + (c + e) % nc))
            for e in range(1, nc)
        ]

    a, b, last = {}, {}, []
    for p in range(2):
        a[p, 0] = first(p, 0)
    line.begin()
    perturb_tiles(sigma, noise, perturb, wide, made, load, store)
    for k in range(nz + 2):
        for p in range(2):
            if 0 < k < nz:
                a[p, k] = first(p, k)
            if 0 <= k - 1 < nz:
                b[p, k - 1] = second(p, k - 1, a[p, k - 1])
            if 0 <= k - 2 < nz:
                last += third(p, k - 2, b[p, k - 2])
        if k >= 3:
            line.relay(k - 2)
    for copy in last:
        copy.wait_recv()
    for copy in sends:
        copy.wait_send()
    line.end()


def spread(pairs, sigma, noise, shard):
    nz, ny, nx = lax.axis_size("dp"), lax.axis_size("mx"), lax.axis_size("my")
    nc = 2 if nx % 2 == 0 else 1
    nx //= nc
    _, _, _, rows, width = pairs.shape
    most = max(nx, ny)
    planes, hid, _ = sigma.shape
    tile = 256 if hid % 256 == 0 else hid
    flat = (planes * hid, width)
    anywhere = pl.BlockSpec(memory_space=pl.ANY)
    within = pl.BlockSpec(memory_space=VMEM)
    bf16 = jnp.bfloat16
    return pl.pallas_call(
        spread_kernel,
        out_shape=[
            jax.ShapeDtypeStruct((2, 2, nz, ny, nx, nc, rows, width), bf16),
            jax.ShapeDtypeStruct(flat, bf16),
            jax.ShapeDtypeStruct((nz,) + shard.shape, bf16),
        ],
        in_specs=[anywhere, anywhere, anywhere, within],
        out_specs=[anywhere, anywhere, within],
        scratch_shapes=[
            DMA((2, nz)), DMA((2, nz)),
            DMA((2, nz, most)), DMA((2, nz, most)),
            DMA((2, nz, most)), DMA((2, nz, most)),
            DMA((2, nz, nc)), DMA((2, nz, nc)),
            DMA((2,)),
            DMA((2, nz)), DMA((2, nz)), DMA,
            VMEM((2, 2, tile, width), bf16),
            VMEM((2, tile, width), bf16),
            DMA((2, 2)), DMA((2,)),
        ],
        compiler_params=pltpu.CompilerParams(
            collective_id=1, has_side_effects=True, vmem_limit_bytes=60 * 2**20
        ),
        cost_estimate=pl.CostEstimate(flops=10**10, bytes_accessed=10**7, transcendentals=0),
        name="spread",
    )(pairs, sigma.reshape(flat), noise.reshape(flat), shard)


def project_kernel(scale, k, half, gathered, means, perturb, signs, shard, out, full, *scratch):
    x, a, m, p, s, part, send, recv, s_sem, r_sem, load, g_s, g_r, g_own = scratch
    line = LineGather(shard, full, g_s, g_r, g_own)
    z, n = lax.axis_index("dp"), lax.axis_size("dp")
    rows, hid = out.shape
    sources = (gathered.at[half, 0], gathered.at[half, 1], means.at[k], perturb.at[k], signs)
    loads = [
        pltpu.make_async_copy(source, target, load.at[i])
        for i, (source, target) in enumerate(zip(sources, (x, a, m, p, s)))
    ]
    for copy in loads:
        copy.start()
    tile = 256 if hid % 256 == 0 else hid
    barrier = pltpu.get_barrier_semaphore()

    @pl.when(z > 0)
    def _():
        pl.semaphore_signal(barrier, inc=1, device_id={"dp": z - 1}, device_id_type=MESH)

    @pl.when(z < n - 1)
    def _():
        pl.semaphore_signal(barrier, inc=1, device_id={"dp": z + 1}, device_id_type=MESH)

    inner = (z > 0) & (z < n - 1)

    @pl.when(inner)
    def _():
        pl.semaphore_wait(barrier, 2)

    @pl.when(jnp.logical_not(inner) & (n > 1))
    def _():
        pl.semaphore_wait(barrier, 1)

    line.begin()
    for copy in loads:
        copy.wait()

    def tiles(body):
        def step(j, carry):
            body(pl.ds(pl.multiple_of(j * tile, tile), tile))
            return carry

        lax.fori_loop(0, hid // tile, step, 0)

    def compute(g):
        span = pl.ds(pl.multiple_of(g * rows, rows), rows)

        def body(cols):
            left = x[span, :]
            mean = dot(left, m[cols, :], ((1,), (1,)))
            pert = dot(left * a[span, :], p[cols, :], ((1,), (1,)))
            part[:, cols] = scale * mean + scale * pert * s[g, :, cols].astype(jnp.float32)

        tiles(body)

    def copy(d, g):
        return remote(
            send.at[g], recv.at[d, g], s_sem.at[g], r_sem.at[d, g], dp=(z + 1 - 2 * d + n) % n
        )

    def slot(i, carry):
        t, d = i // 2, i % 2
        behind = z + d * (n - 1 - 2 * z)
        ahead = n - 1 - behind

        @pl.when((t >= behind) & (ahead > 0))
        def _():
            g = (1 - d) * (n - 1 - t + z) + d * (t - (n - 1 - z))
            compute(g)

            @pl.when(behind > 0)
            def _():
                copy(d, g).wait_recv()

                def body(cols):
                    total = part[:, cols] + recv[d, g, :, cols].astype(jnp.float32)
                    send[g, :, cols] = total.astype(send.dtype)

                tiles(body)

            @pl.when(behind == 0)
            def _():
                def body(cols):
                    send[g, :, cols] = part[:, cols].astype(send.dtype)

                tiles(body)

            copy(d, g).start()

        @pl.when(d == 1)
        def _():
            line.relay(t + 1)

        return carry

    lax.fori_loop(0, 2 * (n - 1), slot, 0)
    compute(z)

    @pl.when(z > 0)
    def _():
        copy(0, z).wait_recv()

        def body(cols):
            part[:, cols] = part[:, cols] + recv[0, z, :, cols].astype(jnp.float32)

        tiles(body)

    @pl.when(z < n - 1)
    def _():
        copy(1, z).wait_recv()

        def body(cols):
            part[:, cols] = part[:, cols] + recv[1, z, :, cols].astype(jnp.float32)

        tiles(body)

    def body(cols):
        out[:, cols] = part[:, cols]

    tiles(body)
    for g in range(n):
        @pl.when(z != g)
        def _():
            copy(0, g).wait_send()

    line.end()


def project(cid, k, half, scale, gathered, means, perturb, signs, shard):
    n = lax.axis_size("dp")
    tokens, width = gathered.shape[2:]
    hid = means.shape[1]
    rows = tokens // n
    return pl.pallas_call(
        functools.partial(project_kernel, scale, k, half),
        out_shape=[
            jax.ShapeDtypeStruct((rows, hid), jnp.float32),
            jax.ShapeDtypeStruct((n, rows, hid), jnp.bfloat16),
        ],
        in_specs=[pl.BlockSpec(memory_space=pl.ANY)] * 4 + [pl.BlockSpec(memory_space=VMEM)],
        out_specs=[pl.BlockSpec(memory_space=VMEM)] * 2,
        scratch_shapes=[
            VMEM((tokens, width), jnp.bfloat16),
            VMEM((tokens, width), jnp.bfloat16),
            VMEM((hid, width), jnp.bfloat16),
            VMEM((hid, width), jnp.bfloat16),
            VMEM((n, rows, hid), jnp.bfloat16),
            VMEM((rows, hid), jnp.float32),
            VMEM((n, rows, hid), jnp.bfloat16),
            VMEM((2, n, rows, hid), jnp.bfloat16),
            DMA((n,)),
            DMA((2, n)),
            DMA((5,)),
            DMA((2, n)),
            DMA((2, n)),
            DMA,
        ],
        compiler_params=pltpu.CompilerParams(
            collective_id=cid, has_side_effects=True, vmem_limit_bytes=60 * 2**20
        ),
        cost_estimate=pl.CostEstimate(flops=2 * 10**10, bytes_accessed=10**7, transcendentals=0),
        name=f"project{k}",
    )(gathered, means, perturb, signs, shard)


def finish_kernel(t, out, a1, rc, rx, ry, b0, b1, r0, r1, fin, s_sem, r_sem):
    (z, y, x, c), (nz, ny, nx, nc) = place()
    width = t.shape[-1]
    half = width // 2
    f32, bf16 = jnp.float32, jnp.bfloat16
    lo, hi = pl.ds(0, half), pl.ds(half, half)
    greet_axes()
    sends = []
    count = [0]

    def start(src, dst, **where):
        i = count[0]
        count[0] += 1
        copy = remote(src, dst, s_sem.at[i], r_sem.at[i], **where)
        copy.start()
        sends.append(copy)
        return copy

    def groups(body):
        def step(g, carry):
            body(g)
            return carry

        lax.fori_loop(0, nz, step, 0)

    wait = [
        start(t.at[:, :, :, (c + e) % nc], rc.at[e - 1], my=x * nc + (c + e) % nc) for e in range(1, nc)
    ]
    for copy in wait:
        copy.wait_recv()

    def add_cores(g):
        for i in range(ny):
            for j in range(nx):
                total = t[g, i, j, c].astype(f32)
                for e in range(nc - 1):
                    total = total + rc[e, g, i, j].astype(f32)
                a1[g, i, j] = total.astype(bf16)

    groups(add_cores)
    wait = [
        start(a1.at[:, :, (x + e) % nx, :, lo], rx.at[e - 1], my=((x + e) % nx) * nc + c)
        for e in range(1, nx)
    ]
    wait += [
        start(a1.at[:, (y + e) % ny, :, :, hi], ry.at[e - 1], mx=(y + e) % ny) for e in range(1, ny)
    ]
    for copy in wait:
        copy.wait_recv()

    def mine(g, i, j, cols):
        total = t[g, i, j, c, :, cols].astype(f32)
        for e in range(nc - 1):
            total = total + rc[e, g, i, j, :, cols].astype(f32)
        return total

    def low(g, i):
        total = mine(g, i, x, lo)
        for e in range(nx - 1):
            total = total + rx[e, g, i].astype(f32)
        return total

    def high(g, j):
        total = mine(g, y, j, hi)
        for e in range(ny - 1):
            total = total + ry[e, g, j].astype(f32)
        return total

    def add_first(g):
        for i in range(ny):
            b0[i, g] = low(g, i).astype(bf16)
        for j in range(nx):
            b1[j, g] = high(g, j).astype(bf16)

    groups(add_first)
    wait = [start(b0.at[(y + e) % ny], r0.at[e - 1], mx=(y + e) % ny) for e in range(1, ny)]
    wait += [
        start(b1.at[(x + e) % nx], r1.at[e - 1], my=((x + e) % nx) * nc + c) for e in range(1, nx)
    ]
    for copy in wait:
        copy.wait_recv()

    def add_second(g):
        total = low(g, y)
        for e in range(ny - 1):
            total = total + r0[e, g].astype(f32)
        fin[g, :, lo] = total.astype(bf16)
        total = high(g, x)
        for e in range(nx - 1):
            total = total + r1[e, g].astype(f32)
        fin[g, :, hi] = total.astype(bf16)

    groups(add_second)
    cols = pl.ds(pl.multiple_of(z * width, width), width)
    wait = [start(fin.at[(z + d) % nz], out.at[:, cols], dp=(z + d) % nz) for d in range(1, nz)]
    out[:, cols] = fin[z]
    for copy in wait:
        copy.wait_recv()
    for copy in sends:
        copy.wait_send()


def finish(cid, total):
    nz, ny, nx = lax.axis_size("dp"), lax.axis_size("mx"), lax.axis_size("my")
    nc = 2 if nx % 2 == 0 else 1
    nx //= nc
    tokens, width = total.shape
    rows = tokens // (nz * ny * nx * nc)
    half = width // 2
    copies = nz + ny * 2 + nx * 2 + nc
    bf16 = jnp.bfloat16
    return pl.pallas_call(
        finish_kernel,
        out_shape=jax.ShapeDtypeStruct((rows, nz * width), bf16),
        in_specs=[pl.BlockSpec(memory_space=VMEM)],
        out_specs=pl.BlockSpec(memory_space=VMEM),
        scratch_shapes=[
            VMEM((nz, ny, nx, rows, width), bf16),
            VMEM((max(nc - 1, 1), nz, ny, nx, rows, width), bf16),
            VMEM((max(nx - 1, 1), nz, ny, rows, half), bf16),
            VMEM((max(ny - 1, 1), nz, nx, rows, half), bf16),
            VMEM((ny, nz, rows, half), bf16),
            VMEM((nx, nz, rows, half), bf16),
            VMEM((max(ny - 1, 1), nz, rows, half), bf16),
            VMEM((max(nx - 1, 1), nz, rows, half), bf16),
            VMEM((nz, rows, width), bf16),
            DMA((copies,)),
            DMA((copies,)),
        ],
        compiler_params=pltpu.CompilerParams(
            collective_id=cid, has_side_effects=True, vmem_limit_bytes=32 * 2**20
        ),
        cost_estimate=pl.CostEstimate(flops=10**10, bytes_accessed=10**7, transcendentals=0),
        name=f"finish{cid}",
    )(total.reshape(nz, ny, nx, nc, rows, width))


def grad_kernel(groups, scale, hid, sign, x, a, noise, *rest):
    mean, sigma = rest[-2:]
    rows = x.shape[0] // groups
    total_mean = total_pert = None
    for g in range(groups):
        part = slice(g * rows, (g + 1) * rows)
        left = hid[part, :]
        right = x[part, :]
        m = (scale * dot(left, right, ((0,), (0,)))).astype(jnp.bfloat16)
        p = (scale * dot(left * sign[part, :], right * a[part, :], ((0,), (0,)))).astype(jnp.bfloat16)
        m, p = m.astype(jnp.float32), p.astype(jnp.float32)
        total_mean = m if g == 0 else total_mean + m
        total_pert = p if g == 0 else total_pert + p
    mean[...] = total_mean.astype(jnp.bfloat16)
    sigma[...] = (total_pert * noise[...].astype(jnp.float32)).astype(jnp.bfloat16)


def weight_grads(groups, k, half, scale, hid, sign, gathered, noise, into):
    tokens, ff = hid.shape
    width = gathered.shape[3]
    tile = 256 if ff % 256 == 0 else ff
    whole = lambda j: pl.BlockSpec((None, None, tokens, width), lambda i: (half, j, 0, 0))
    block = pl.BlockSpec((None, tile, width), lambda i: (k, i, 0))
    cols = pl.BlockSpec((tokens, tile), lambda i: (0, i))
    keep = [pl.BlockSpec(memory_space=pl.ANY)] * len(into)
    return pl.pallas_call(
        functools.partial(grad_kernel, groups, scale),
        grid=(ff // tile,),
        out_shape=[jax.ShapeDtypeStruct(noise.shape, jnp.bfloat16)] * 2,
        in_specs=[cols, cols, whole(0), whole(1), block] + keep,
        out_specs=[block, block],
        input_output_aliases={5 + i: i for i in range(len(into))},
        cost_estimate=pl.CostEstimate(
            flops=4 * tokens * ff * width, bytes_accessed=6 * ff * width, transcendentals=0
        ),
        name=f"grads{k}",
    )(hid, sign, gathered, gathered, noise, *into)


def on_device(
    inputs,
    weight_means,
    weight_sigmas,
    weight_noise,
    input_signs,
    output_signs,
    hidden_signs,
    result_signs,
    cotangent,
):
    f32, bf16 = jnp.float32, jnp.bfloat16
    scale_in = D ** (-0.5)
    scale_out = FF ** (-0.5)
    groups = lax.axis_size("dp")

    def share(value):
        return lax.all_gather(value, "dp", axis=0, tiled=True)

    rows, full = inputs.shape
    width = full // groups
    pairs = jnp.stack([inputs, to_sign(input_signs), cotangent, to_sign(result_signs)])
    pairs = pairs.reshape(2, 2, rows, groups, width).swapaxes(2, 3)
    own_s0, own_s1 = to_sign(output_signs[0]).T, to_sign(output_signs[1]).T
    own_s2 = to_sign(hidden_signs).T
    gathered, perturb, s0 = spread(pairs, weight_sigmas, weight_noise, own_s0)
    gathered = gathered.reshape(2, 2, -1, width)
    perturb = perturb.reshape(weight_sigmas.shape)
    a, r = gathered[0, 1], gathered[1, 1]

    gate, s1 = project(2, 0, 0, scale_in, gathered, weight_means, perturb, s0, own_s1)
    up, s2 = project(3, 1, 0, scale_in, gathered, weight_means, perturb, s1, own_s2)
    gate_sig = jax.nn.sigmoid(gate)
    hidden = (gate * gate_sig * up).astype(bf16)
    hid_grad, hidden = project(4, 2, 1, scale_out, gathered, weight_means, perturb, s2, hidden)
    up_grad = share((hid_grad * gate * gate_sig).astype(bf16))
    gate_grad = share(
        (hid_grad * up * gate_sig * (1.0 + gate * (1.0 - gate_sig))).astype(bf16)
    )
    hidden, s0, s1, s2 = (v.reshape(-1, v.shape[2]) for v in (hidden, s0, s1, s2))

    def back(k, value, sign):
        return (
            dot(value, weight_means[k], ((1,), (0,))),
            dot(value * sign, perturb[k], ((1,), (0,))),
        )

    mean, pert = back(2, hidden, s2)
    result = finish(5, (scale_out * mean + scale_out * pert * r.astype(f32)).astype(bf16))
    grads = weight_grads(groups, 2, 1, scale_out, hidden, s2, gathered, weight_noise, ())
    up_grad, result, *grads = lax.optimization_barrier((up_grad, result, *grads))
    up_mean, up_pert = back(1, up_grad, s1)
    grads = weight_grads(groups, 1, 0, scale_in, up_grad, s1, gathered, weight_noise, grads)
    gate_grad, up_mean, up_pert, *grads = lax.optimization_barrier(
        (gate_grad, up_mean, up_pert, *grads)
    )
    gate_mean, gate_pert = back(0, gate_grad, s0)
    input_grad = finish(
        6,
        (
            scale_in * (gate_mean + up_mean) + scale_in * (gate_pert + up_pert) * a.astype(f32)
        ).astype(bf16),
    )
    mean_grad, sigma_grad = weight_grads(
        groups, 0, 0, scale_in, gate_grad, s0, gathered, weight_noise, grads
    )
    return (result, input_grad, mean_grad, sigma_grad)


def solution(mesh):
    return jax.shard_map(
        on_device,
        mesh=mesh,
        in_specs=(
            P(("dp", "mx", "my"), None),
            P(None, ("mx", "my"), "dp"),
            P(None, ("mx", "my"), "dp"),
            P(None, ("mx", "my"), "dp"),
            P(("dp", "mx", "my"), None),
            P(None, ("mx", "my"), "dp"),
            P(("mx", "my"), "dp"),
            P(("dp", "mx", "my"), None),
            P(("dp", "mx", "my"), None),
        ),
        out_specs=(
            P(("dp", "mx", "my"), None),
            P(("dp", "mx", "my"), None),
            P(None, ("mx", "my"), "dp"),
            P(None, ("mx", "my"), "dp"),
        ),
        check_vma=False,
    )
```

time: 731 us -> 473 us (0.65); the launches traced: 721 us -> 472 us
  waiting for transfers between devices: 465 us -> 36.5 us
  Pallas kernels: 39.9 us -> 364 us
  matrix products: 74.7 us -> 38.3 us
  local copies, waits for them, and re-layouts: 35.1 us -> 3.26 us
  blocking collectives: 31.6 us -> 0 us
  other arithmetic: 39.6 us -> 15.8 us
  starting transfers between devices: 20.3 us -> 0.08 us
    pallas_call x1 -> x9, Pallas kernels: 39.9 us -> 364 us  [the longest x3 193 us: project(): pl.pallas_call(functools.partial(project_kernel, scale, k, half), out_sha...]
    all_gather x5 -> x2, waiting for transfers between devices: 268 us -> 35.7 us  [share(): return lax.all_gather(value, 'dp', axis=0, tiled=True)]
    reduce_scatter x3 -> x0, waiting for transfers between devices: 153 us -> none  [project(): lax.psum_scatter(total.astype(bf16), 'dp', scatter_dimension=0, tiled=True)]
    unnamed x12 -> x2, waiting for transfers between devices: 39.6 us -> 0.71 us
    dot_general x12 -> x6, matrix products: 74.7 us -> 38.3 us  [dot(): lax.dot_general(left, right, (dims, ((), ())), preferred_element_type=jnp...]
    all_to_all x2 -> x0, blocking collectives: 31.6 us -> none  [spread(): lax.all_to_all(both.reshape(2, 1, rows, width), 'dp', split_axis=3, conca...]
    unnamed x36 -> x26, local copies, waits for them, and re-layouts: 22.6 us -> 1.57 us
    convert_element_type x2, other arithmetic: 17.2 us -> 6.65 us  [the longest x1 4.08 us: on_device(): (hid_grad * up * gate_sig * (1.0 + gate * (1.0 - gate_sig))).astype(bf16)]
  transfers between devices with their start and end apart: 12 -> 2, of which waited for: 10 -> 2; matrix products, arithmetic and copies ran while one was open for 18% -> 6% of each run, Pallas kernels for 6% -> 11%
where the time goes in v1:
time: 473 us; the launch traced here: 472 us
  Pallas kernels  364 us (77%)
  matrix products  38.3 us (8%)
  waiting for transfers between devices  36.5 us (8%)
  other arithmetic  15.8 us (3%)
  between operations  14.2 us (3%)
    pallas_call x3, Pallas kernels, project(): pl.pallas_call(functools.partial(project_kernel, scale, k, half), out_sha...  193 us
    pallas_call x1, Pallas kernels, spread(): pl.pallas_call(spread_kernel, out_shape=[jax.ShapeDtypeStruct((2, 2, nz,...  83.9 us
    pallas_call x3, Pallas kernels, weight_grads(): pl.pallas_call(functools.partial(grad_kernel, groups, scale), grid=(ff //...  45 us
    pallas_call x2, Pallas kernels, finish(): pl.pallas_call(finish_kernel, out_shape=jax.ShapeDtypeStruct((rows, nz *...  42.6 us
    dot_general x6, matrix products, dot(): lax.dot_general(left, right, (dims, ((), ())), preferred_element_type=jnp...  38.3 us
    all_gather x2, waiting for transfers between devices, share(): return lax.all_gather(value, 'dp', axis=0, tiled=True)  35.7 us
  transfers between devices with their start and end apart: 2, of which 2 were waited for; matrix products, arithmetic and copies ran while one was open for 6% of the time, Pallas kernels for 11%

profile of v1, /device:TPU:0, one launch (start us, length us, event | category | flops | bytes accessed | tf_op | source)
XLA Modules:
  0.0 472.1 jit_solution(6184073620532097241)
XLA Ops:
  7.2 0.0 all-gather.3.cloned.1.call-start
  7.2 1.2 fusion.28
  8.4 1.1 pad_maximum_fusion
  9.5 0.6 reshape.62
  10.1 1.1 copy.19
  11.3 3.1 fusion.26
  14.4 1.1 fusion.27.shard
  15.5 83.9 %spread.1 = (bf16[2,2,4,2,2,2,24,1024]{7,6,5,4,3,2,1,0:T(8,128)(2,1)}, bf16[5376,1024]{1,0:T(8,128)(2,1)}, bf16[4,192,1792]{2,1,0:T(8,128)(2,1)}) custom-call(bf16[2,2,4,24,1024]{4,3,2,1,0:T(8,128)(2,1)} %bitcast.77, bf16[5376,1024]{1,0:T(8,128)(2,1)} %bitcast.80, bf16[5376,1024]{1,0:T(8,128)(2,1)} %bitcast.68, bf16[192,1792]{1,0:T(8,128)(2,1)} %get-tuple-element.55.shard), custom_call_target="tpu_custom_call" | custom-call | flops 10000000000 | bytes 10000000 | tf_op jit(solution)/shard_map/spread/pallas_call | solution.py:249
  99.4 66.0 %project0.1 = (f32[192,1792]{1,0:T(8,128)}, bf16[4,192,1792]{2,1,0:T(8,128)(2,1)}) custom-call(bf16[2,2,768,1024]{3,2,1,0:T(8,128)(2,1)} %bitcast.57, bf16[3,1792,1024]{2,1,0:T(8,128)(2,1)} %means.5, bf16[3,1792,1024]{2,1,0:T(8,128)(2,1)} %bitcast.81, bf16[4,192,1792]{2,1,0:T(8,128)(2,1)} %get-tuple-element.30.signs, bf16[192,1792]{1,0:T(8,128)(2,1)} %get-tuple-element.54.shard), custom_call_target="tpu_custom_call" | custom-call | flops 20000000000 | bytes 10000000 | tf_op jit(solution)/shard_map/project0/pallas_call | solution.py:410
  165.4 66.5 %project1.1 = (f32[192,1792]{1,0:T(8,128)}, bf16[4,192,1792]{2,1,0:T(8,128)(2,1)}) custom-call(bf16[2,2,768,1024]{3,2,1,0:T(8,128)(2,1)} %bitcast.58, bf16[3,1792,1024]{2,1,0:T(8,128)(2,1)} %means.5, bf16[3,1792,1024]{2,1,0:T(8,128)(2,1)} %bitcast.82, bf16[4,192,1792]{2,1,0:T(8,128)(2,1)} %get-tuple-element.31.signs, bf16[192,1792]{1,0:T(8,128)(2,1)} %fusion.27.shard), custom_call_target="tpu_custom_call" | custom-call | flops 20000000000 | bytes 10000000 | tf_op jit(solution)/shard_map/project1/pallas_call | solution.py:410
  231.9 2.6 multiply_convert_fusion.2.shard
  234.4 60.1 %project2.1 = (f32[192,1792]{1,0:T(8,128)}, bf16[4,192,1792]{2,1,0:T(8,128)(2,1)}) custom-call(bf16[2,2,768,1024]{3,2,1,0:T(8,128)(2,1)} %bitcast.59, bf16[3,1792,1024]{2,1,0:T(8,128)(2,1)} %means.5, bf16[3,1792,1024]{2,1,0:T(8,128)(2,1)} %bitcast.83, bf16[4,192,1792]{2,1,0:T(8,128)(2,1)} %get-tuple-element.32.signs, ...), custom_call_target="tpu_custom_call" | custom-call | flops 20000000000 | bytes 10000000 | tf_op jit(solution)/shard_map/project2/pallas_call | solution.py:410
  294.6 4.1 multiply_convert_fusion
  298.7 0.0 all-gather.5.cloned.1.call-start
  298.7 0.7 all-gather.5.cloned.1.call-update
  299.4 6.8 %fusion.4 = f32[768,1024]{1,0:T(8,128)} fusion(bf16[768,1792]{1,0:T(8,128)(2,1)S(1)} %bitcast.71, bf16[3,1792,1024]{2,1,0:T(8,128)(2,1)} %means.5), kind=kOutput, calls=%fused_computation.4 | convolution fusion | flops 2818572288 | bytes 9568256 | tf_op jit(solution)/shard_map/dot_general | solution.py:22
  306.2 15.3 %grads2.1 = (bf16[3,1792,1024]{2,1,0:T(8,128)(2,1)}, bf16[3,1792,1024]{2,1,0:T(8,128)(2,1)}) custom-call(bf16[768,1792]{1,0:T(8,128)(2,1)} %bitcast.70, bf16[768,1792]{1,0:T(8,128)(2,1)} %bitcast.69, bf16[2,2,768,1024]{3,2,1,0:T(8,128)(2,1)} %bitcast.60, bf16[2,2,768,1024]{3,2,1,0:T(8,128)(2,1)} %bitcast.61, bf16[3,1792,1024]{2,1,0:T(8,128)(2,1)} %noise.5), custom_call_target="tpu_custom_call" | custom-call | flops 5637144576 | bytes 11010048 | tf_op jit(solution)/shard_map/grads2/pallas_call | solution.py:604
  321.5 2.6 mul.81
  324.1 0.2 copy-done.11
  324.3 5.7 %fusion.18 = bf16[768,1024]{1,0:T(8,128)(2,1)S(1)} fusion(f32[768,1024]{1,0:T(8,128)S(1)} %copy-done.11, bf16[768,1792]{1,0:T(8,128)(2,1)S(1)} %bitcast.72, bf16[5376,1024]{1,0:T(8,128)(2,1)} %get-tuple-element.29, bf16[2,2,768,1024]{3,2,1,0:T(8,128)(2,1)} %bitcast.62), kind=kOutput, calls=%fused_computation.20 | convolution fusion | flops 2823290880 | bytes 12713984 | tf_op jit(solution)/shard_map/dot_general | solution.py:22
  330.0 22.0 %finish5.1 = bf16[24,4096]{1,0:T(8,128)(2,1)S(1)} custom-call(bf16[4,2,2,2,24,1024]{5,4,3,2,1,0:T(8,128)(2,1)S(1)} %bitcast.56), custom_call_target="tpu_custom_call" | custom-call | flops 10000000000 | bytes 10000000 | tf_op jit(solution)/shard_map/finish5/pallas_call | solution.py:553
  352.0 7.2 %all-gather.3.cloned.1.call-done.hid = bf16[768,1792]{1,0:T(8,128)(2,1)} async-done(((bf16[192,1792]{1,0:T(8,128)(2,1)}), bf16[768,1792]{1,0:T(8,128)(2,1)}) %all-gather.3.cloned.1.call-update) | async-done | bytes 2752528 | tf_op jit(solution)/shard_map/all_gather | solution.py:635
  359.3 14.9 %grads1.1 = (bf16[3,1792,1024]{2,1,0:T(8,128)(2,1)}, bf16[3,1792,1024]{2,1,0:T(8,128)(2,1)}) custom-call(bf16[768,1792]{1,0:T(8,128)(2,1)} %all-gather.3.cloned.1.call-done.hid, bf16[768,1792]{1,0:T(8,128)(2,1)} %bitcast.75, bf16[2,2,768,1024]{3,2,1,0:T(8,128)(2,1)} %bitcast.63, ...), custom_call_target="tpu_custom_call", output_to_operand_aliasing={{0}: (5, {}), {1}: (6, {})} | custom-call | flops 5637144576 | bytes 11010048 | tf_op jit(solution)/shard_map/grads1/pallas_call | solution.py:604
  374.2 6.9 %fusion.2 = f32[768,1024]{1,0:T(8,128)} fusion(bf16[768,1792]{1,0:T(8,128)(2,1)S(1)} %copy-done.6, bf16[3,1792,1024]{2,1,0:T(8,128)(2,1)} %means.5), kind=kOutput, calls=%fused_computation.2 | convolution fusion | flops 2818572288 | bytes 9568256 | tf_op jit(solution)/shard_map/dot_general | solution.py:22
  381.0 6.8 %fusion.9 = f32[768,1024]{1,0:T(8,128)} fusion(bf16[5376,1024]{1,0:T(8,128)(2,1)} %get-tuple-element.29, bf16[768,1792]{1,0:T(8,128)(2,1)S(1)} %copy-done.7, bf16[768,1792]{1,0:T(8,128)(2,1)S(1)} %bitcast.76), kind=kOutput, calls=%fused_computation.9 | convolution fusion | flops 2819948544 | bytes 12320768 | tf_op jit(solution)/shard_map/dot_general | solution.py:22
  387.9 28.5 %all-gather.5.cloned.1.call-done.hid = bf16[768,1792]{1,0:T(8,128)(2,1)} async-done(((bf16[192,1792]{1,0:T(8,128)(2,1)}), bf16[768,1792]{1,0:T(8,128)(2,1)}) %all-gather.5.cloned.1.call-update) | async-done | bytes 2752528 | tf_op jit(solution)/shard_map/all_gather | solution.py:635
  416.4 6.0 %fusion.6 = f32[768,1024]{1,0:T(8,128)S(1)} fusion(bf16[5376,1024]{1,0:T(8,128)(2,1)} %get-tuple-element.29, bf16[768,1792]{1,0:T(8,128)(2,1)} %all-gather.5.cloned.1.call-done.hid, bf16[768,1792]{1,0:T(8,128)(2,1)S(1)} %bitcast.74), kind=kOutput, calls=%fused_computation.6 | convolution fusion | flops 2819948544 | bytes 12320768 | tf_op jit(solution)/shard_map/dot_general | solution.py:22
  422.4 6.2 %fusion.16 = bf16[768,1024]{1,0:T(8,128)(2,1)S(1)} fusion(f32[768,1024]{1,0:T(8,128)S(1)} %fusion.6, f32[768,1024]{1,0:T(8,128)S(1)} %copy-done.9, f32[768,1024]{1,0:T(8,128)S(1)} %copy-done.10, bf16[768,1792]{1,0:T(8,128)(2,1)S(1)} %copy-done.5, bf16[3,1792,1024]{2,1,0:T(8,128)(2,1)} %means.5, bf16[2,2,768,1024]{3,2,1,0:T(8,128)(2,1)} %bitcast.65), kind=kOutput, calls=%fused_computation.17 | convolution fusion | flops 2824863744 | bytes 19005440 | tf_op jit(solution)/shard_map/dot_general | solution.py:22
  428.6 20.5 %finish6.1 = bf16[24,4096]{1,0:T(8,128)(2,1)S(1)} custom-call(bf16[4,2,2,2,24,1024]{5,4,3,2,1,0:T(8,128)(2,1)S(1)} %bitcast.55), custom_call_target="tpu_custom_call" | custom-call | flops 10000000000 | bytes 10000000 | tf_op jit(solution)/shard_map/finish6/pallas_call | solution.py:553
  449.2 14.8 %grads0.1 = (bf16[3,1792,1024]{2,1,0:T(8,128)(2,1)}, bf16[3,1792,1024]{2,1,0:T(8,128)(2,1)}) custom-call(bf16[768,1792]{1,0:T(8,128)(2,1)} %all-gather.5.cloned.1.call-done.hid, bf16[768,1792]{1,0:T(8,128)(2,1)} %bitcast.73, bf16[2,2,768,1024]{3,2,1,0:T(8,128)(2,1)} %bitcast.66, ...), custom_call_target="tpu_custom_call", output_to_operand_aliasing={{0}: (5, {}), {1}: (6, {})} | custom-call | flops 5637144576 | bytes 11010048 | tf_op jit(solution)/shard_map/grads0/pallas_call | solution.py:604
  464.0 0.7 copy.26
  464.6 0.7 copy.27
  (24 shorter events, 0.1 us)
Async XLA Ops:
  7.2 352.1 %all-gather.3.cloned.1.call-start = ((), (), s32[]{:S(2)}) async-start(), calls=%async_computation | async-start | bytes 3440640 | tf_op jit(solution)/shard_map/all_gather | solution.py:635
  10.1 4.3 copy-start.8
  165.4 66.5 %copy-start.2 = (f32[192,1792]{1,0:T(8,128)S(1)}, f32[192,1792]{1,0:T(8,128)}, u32[]{:S(2)}) copy-start(f32[192,1792]{1,0:T(8,128)} %get-tuple-element.33) | copy-start | bytes 4128772
  294.5 4.9 %copy-start.1 = (bf16[4,192,1792]{2,1,0:T(8,128)(2,1)S(1)}, bf16[4,192,1792]{2,1,0:T(8,128)(2,1)}, u32[]{:S(2)}) copy-start(bf16[4,192,1792]{2,1,0:T(8,128)(2,1)} %get-tuple-element.36) | copy-start | bytes 8257540
  298.7 117.7 %all-gather.5.cloned.1.call-start = ((), (), s32[]{:S(2)}) async-start(), calls=%async_computation.1 | async-start | bytes 3440640 | tf_op jit(solution)/shard_map/all_gather | solution.py:635
  306.2 15.4 %copy-start = (bf16[4,192,1792]{2,1,0:T(8,128)(2,1)S(1)}, bf16[4,192,1792]{2,1,0:T(8,128)(2,1)}, u32[]{:S(2)}) copy-start(bf16[4,192,1792]{2,1,0:T(8,128)(2,1)} %get-tuple-element.32.signs) | copy-start | bytes 8257540
  321.5 2.8 copy-start.11
  359.3 14.9 %copy-start.6 = (bf16[768,1792]{1,0:T(8,128)(2,1)S(1)}, bf16[768,1792]{1,0:T(8,128)(2,1)}, u32[]{:S(2)}) copy-start(bf16[768,1792]{1,0:T(8,128)(2,1)} %all-gather.3.cloned.1.call-done.hid) | copy-start | bytes 8257540
  374.2 6.9 %copy-start.4 = (bf16[4,192,1792]{2,1,0:T(8,128)(2,1)S(1)}, bf16[4,192,1792]{2,1,0:T(8,128)(2,1)}, u32[]{:S(2)}) copy-start(bf16[4,192,1792]{2,1,0:T(8,128)(2,1)} %get-tuple-element.31.signs) | copy-start | bytes 8257540
  374.2 6.9 %copy-start.7 = (bf16[768,1792]{1,0:T(8,128)(2,1)S(1)}, bf16[768,1792]{1,0:T(8,128)(2,1)}, u32[]{:S(2)}) copy-start(bf16[768,1792]{1,0:T(8,128)(2,1)} %all-gather.3.cloned.1.call-done.hid) | copy-start | bytes 8257540
  381.0 35.3 %copy-start.3 = (bf16[4,192,1792]{2,1,0:T(8,128)(2,1)S(1)}, bf16[4,192,1792]{2,1,0:T(8,128)(2,1)}, u32[]{:S(2)}) copy-start(bf16[4,192,1792]{2,1,0:T(8,128)(2,1)} %get-tuple-element.30.signs) | copy-start | bytes 8257540
  416.4 6.0 %copy-start.5 = (bf16[768,1792]{1,0:T(8,128)(2,1)S(1)}, bf16[768,1792]{1,0:T(8,128)(2,1)}, u32[]{:S(2)}) copy-start(bf16[768,1792]{1,0:T(8,128)(2,1)} %all-gather.5.cloned.1.call-done.hid) | copy-start | bytes 8257540
  416.4 6.0 %copy-start.9 = (f32[768,1024]{1,0:T(8,128)S(1)}, f32[768,1024]{1,0:T(8,128)}, u32[]{:S(2)}) copy-start(f32[768,1024]{1,0:T(8,128)} %fusion.9) | copy-start | bytes 9437188
  416.4 6.0 %copy-start.10 = (f32[768,1024]{1,0:T(8,128)S(1)}, f32[768,1024]{1,0:T(8,128)}, u32[]{:S(2)}) copy-start(f32[768,1024]{1,0:T(8,128)} %fusion.2) | copy-start | bytes 9437188
Sparse Core Ops, SparseCore 0:
  298.8 60.4 all-gather.2
  360.8 55.4 all-gather.4

commit v2 on v1

--- a/solution.py
+++ b/solution.py
@@ -217,16 +217,23 @@
         a[p, 0] = first(p, 0)
     line.begin()
     perturb_tiles(sigma, noise, perturb, wide, made, load, store)
-    for k in range(nz + 2):
+    for k in range(1, nz):
         for p in range(2):
-            if 0 < k < nz:
-                a[p, k] = first(p, k)
-            if 0 <= k - 1 < nz:
-                b[p, k - 1] = second(p, k - 1, a[p, k - 1])
-            if 0 <= k - 2 < nz:
-                last += third(p, k - 2, b[p, k - 2])
-        if k >= 3:
-            line.relay(k - 2)
+            a[p, k] = first(p, k)
+    for p in range(2):
+        b[p, 0] = second(p, 0, a[p, 0])
+    line.relay(1)
+    for k in range(1, nz):
+        for p in range(2):
+            b[p, k] = second(p, k, a[p, k])
+    for p in range(2):
+        last += third(p, 0, b[p, 0])
+    line.relay(2)
+    for k in range(1, nz):
+        for p in range(2):
+            last += third(p, k, b[p, k])
+    for step in range(3, nz):
+        line.relay(step)
     for copy in last:
         copy.wait_recv()
     for copy in sends:
@@ -593,25 +600,27 @@
     sigma[...] = (total_pert * noise[...].astype(jnp.float32)).astype(jnp.bfloat16)
 
 
-def weight_grads(groups, k, half, scale, hid, sign, gathered, noise, into):
+def weight_grads(groups, k, half, scale, hid, sign, gathered, noise, into, begin=0):
     tokens, ff = hid.shape
     width = gathered.shape[3]
-    tile = 256 if ff % 256 == 0 else ff
+    tile = 256 if ff % 256 == 0 and begin % 256 == 0 else ff
+    skip = begin // tile
     whole = lambda j: pl.BlockSpec((None, None, tokens, width), lambda i: (half, j, 0, 0))
-    block = pl.BlockSpec((None, tile, width), lambda i: (k, i, 0))
+    block = pl.BlockSpec((None, tile, width), lambda i: (k, skip + i, 0))
     cols = pl.BlockSpec((tokens, tile), lambda i: (0, i))
+    signs = pl.BlockSpec((tokens, tile), lambda i: (0, skip + i))
     keep = [pl.BlockSpec(memory_space=pl.ANY)] * len(into)
     return pl.pallas_call(
         functools.partial(grad_kernel, groups, scale),
         grid=(ff // tile,),
         out_shape=[jax.ShapeDtypeStruct(noise.shape, jnp.bfloat16)] * 2,
-        in_specs=[cols, cols, whole(0), whole(1), block] + keep,
+        in_specs=[cols, signs, whole(0), whole(1), block] + keep,
         out_specs=[block, block],
         input_output_aliases={5 + i: i for i in range(len(into))},
         cost_estimate=pl.CostEstimate(
             flops=4 * tokens * ff * width, bytes_accessed=6 * ff * width, transcendentals=0
         ),
-        name=f"grads{k}",
+        name=f"grads{k}_{skip}",
     )(hid, sign, gathered, gathered, noise, *into)
 
 
@@ -651,15 +660,17 @@
     hidden = (gate * gate_sig * up).astype(bf16)
     hid_grad, hidden = project(4, 2, 1, scale_out, gathered, weight_means, perturb, s2, hidden)
     up_grad = share((hid_grad * gate * gate_sig).astype(bf16))
-    gate_grad = share(
-        (hid_grad * up * gate_sig * (1.0 + gate * (1.0 - gate_sig))).astype(bf16)
-    )
+    gate_grad = (hid_grad * up * gate_sig * (1.0 + gate * (1.0 - gate_sig))).astype(bf16)
+    ff = gate_grad.shape[1]
+    cut = -(-ff // 512) * 256 if ff % 256 == 0 else ff
+    spans = [slice(0, cut), slice(cut, ff)] if cut < ff else [slice(0, ff)]
+    gate_grads = [share(gate_grad[:, span]) for span in spans]
     hidden, s0, s1, s2 = (v.reshape(-1, v.shape[2]) for v in (hidden, s0, s1, s2))
 
-    def back(k, value, sign):
+    def back(k, value, sign, span=slice(None)):
         return (
-            dot(value, weight_means[k], ((1,), (0,))),
-            dot(value * sign, perturb[k], ((1,), (0,))),
+            dot(value, weight_means[k, span], ((1,), (0,))),
+            dot(value * sign[:, span], perturb[k, span], ((1,), (0,))),
         )
 
     mean, pert = back(2, hidden, s2)
@@ -668,19 +679,19 @@
     up_grad, result, *grads = lax.optimization_barrier((up_grad, result, *grads))
     up_mean, up_pert = back(1, up_grad, s1)
     grads = weight_grads(groups, 1, 0, scale_in, up_grad, s1, gathered, weight_noise, grads)
-    gate_grad, up_mean, up_pert, *grads = lax.optimization_barrier(
-        (gate_grad, up_mean, up_pert, *grads)
-    )
-    gate_mean, gate_pert = back(0, gate_grad, s0)
-    input_grad = finish(
-        6,
-        (
-            scale_in * (gate_mean + up_mean) + scale_in * (gate_pert + up_pert) * a.astype(f32)
-        ).astype(bf16),
-    )
-    mean_grad, sigma_grad = weight_grads(
-        groups, 0, 0, scale_in, gate_grad, s0, gathered, weight_noise, grads
-    )
+    mean, pert = up_mean, up_pert
+    for span, value in zip(spans, gate_grads):
+        value, mean, pert, *grads = lax.optimization_barrier((value, mean, pert, *grads))
+        gate_mean, gate_pert = back(0, value, s0, span)
+        mean, pert = mean + gate_mean, pert + gate_pert
+        if span.stop == ff:
+            input_grad = finish(
+                6, (scale_in * mean + scale_in * pert * a.astype(f32)).astype(bf16)
+            )
+        grads = weight_grads(
+            groups, 0, 0, scale_in, value, s0, gathered, weight_noise, grads, span.start
+        )
+    mean_grad, sigma_grad = grads
     return (result, input_grad, mean_grad, sigma_grad)
 
 

time: 473 us -> 463 us (0.979)
  waiting for transfers between devices: 36.5 us -> 21.9 us
  matrix products: 38.3 us -> 46.4 us
  Pallas kernels: 364 us -> 358 us
    all_gather x2 -> x3, waiting for transfers between devices: 35.7 us -> 21.8 us  [share(): return lax.all_gather(value, 'dp', axis=0, tiled=True)]
    pallas_call x1, Pallas kernels: 83.9 us -> 71.8 us  [spread(): pl.pallas_call(spread_kernel, out_shape=[jax.ShapeDtypeStruct((2, 2, nz,...]
    dot_general x6 -> x8, matrix products: 38.3 us -> 46.4 us  [dot(): lax.dot_general(left, right, (dims, ((), ())), preferred_element_type=jnp...]
    pallas_call x3 -> x4, Pallas kernels: 45 us -> 48 us  [weight_grads(): pl.pallas_call(functools.partial(grad_kernel, groups, scale), grid=(ff //...]
  transfers between devices with their start and end apart: 2 -> 3, of which waited for: 2 -> 3; matrix products, arithmetic and copies ran while one was open for 6% -> 10% of each run, Pallas kernels for 11% -> 13%
where the time goes in v2:
time: 463 us; the launch traced here: 462 us
  Pallas kernels  358 us (77%)
  matrix products  46.4 us (10%)
  waiting for transfers between devices  21.9 us (5%)
  other arithmetic  16 us (3%)
  between operations  13.9 us (3%)
  local copies, waits for them, and re-layouts  5.55 us (1%)
    pallas_call x3, Pallas kernels, project(): pl.pallas_call(functools.partial(project_kernel, scale, k, half), out_sha...  197 us
    pallas_call x1, Pallas kernels, spread(): pl.pallas_call(spread_kernel, out_shape=[jax.ShapeDtypeStruct((2, 2, nz,...  71.8 us
    pallas_call x4, Pallas kernels, weight_grads(): pl.pallas_call(functools.partial(grad_kernel, groups, scale), grid=(ff //...  48 us
    dot_general x8, matrix products, dot(): lax.dot_general(left, right, (dims, ((), ())), preferred_element_type=jnp...  46.4 us
    pallas_call x2, Pallas kernels, finish(): pl.pallas_call(finish_kernel, out_shape=jax.ShapeDtypeStruct((rows, nz *...  41.9 us
    all_gather x3, waiting for transfers between devices, share(): return lax.all_gather(value, 'dp', axis=0, tiled=True)  21.8 us
  transfers between devices with their start and end apart: 3, of which 3 were waited for; matrix products, arithmetic and copies ran while one was open for 10% of the time, Pallas kernels for 13%

profile of v2, /device:TPU:0, one launch (start us, length us, event | category | flops | bytes accessed | tf_op | source)
XLA Modules:
  0.0 462.1 jit_solution(3342652214117185405)
XLA Ops:
  7.2 1.2 fusion.31
  8.4 1.1 pad_maximum_fusion
  10.1 1.1 copy.21
  11.3 3.1 fusion.29
  14.4 1.0 fusion.30.shard
  15.4 71.8 %spread.1 = (bf16[2,2,4,2,2,2,24,1024]{7,6,5,4,3,2,1,0:T(8,128)(2,1)}, bf16[5376,1024]{1,0:T(8,128)(2,1)}, bf16[4,192,1792]{2,1,0:T(8,128)(2,1)}) custom-call(bf16[2,2,4,24,1024]{4,3,2,1,0:T(8,128)(2,1)} %bitcast.93, bf16[5376,1024]{1,0:T(8,128)(2,1)} %bitcast.101, bf16[5376,1024]{1,0:T(8,128)(2,1)} %bitcast.82, bf16[192,1792]{1,0:T(8,128)(2,1)} %get-tuple-element.69.shard), custom_call_target="tpu_custom_call" | custom-call | flops 10000000000 | bytes 10000000 | tf_op jit(solution)/shard_map/spread/pallas_call | solution.py:256
  87.3 64.7 %project0.1 = (f32[192,1792]{1,0:T(8,128)}, bf16[4,192,1792]{2,1,0:T(8,128)(2,1)}) custom-call(bf16[2,2,768,1024]{3,2,1,0:T(8,128)(2,1)} %bitcast.69, bf16[3,1792,1024]{2,1,0:T(8,128)(2,1)} %means.5, bf16[3,1792,1024]{2,1,0:T(8,128)(2,1)} %bitcast.94, bf16[4,192,1792]{2,1,0:T(8,128)(2,1)} %get-tuple-element.37.signs, bf16[192,1792]{1,0:T(8,128)(2,1)} %get-tuple-element.68.shard), custom_call_target="tpu_custom_call" | custom-call | flops 20000000000 | bytes 10000000 | tf_op jit(solution)/shard_map/project0/pallas_call | solution.py:417
  152.0 66.0 %project1.1 = (f32[192,1792]{1,0:T(8,128)}, bf16[4,192,1792]{2,1,0:T(8,128)(2,1)}) custom-call(bf16[2,2,768,1024]{3,2,1,0:T(8,128)(2,1)} %bitcast.70, bf16[3,1792,1024]{2,1,0:T(8,128)(2,1)} %means.5, bf16[3,1792,1024]{2,1,0:T(8,128)(2,1)} %bitcast.95, bf16[4,192,1792]{2,1,0:T(8,128)(2,1)} %get-tuple-element.38.signs, bf16[192,1792]{1,0:T(8,128)(2,1)} %fusion.30.shard), custom_call_target="tpu_custom_call" | custom-call | flops 20000000000 | bytes 10000000 | tf_op jit(solution)/shard_map/project1/pallas_call | solution.py:417
  218.0 2.6 multiply_convert_fusion.2.shard
  220.6 66.0 %project2.1 = (f32[192,1792]{1,0:T(8,128)}, bf16[4,192,1792]{2,1,0:T(8,128)(2,1)}) custom-call(bf16[2,2,768,1024]{3,2,1,0:T(8,128)(2,1)} %bitcast.71, bf16[3,1792,1024]{2,1,0:T(8,128)(2,1)} %means.5, bf16[3,1792,1024]{2,1,0:T(8,128)(2,1)} %bitcast.96, bf16[4,192,1792]{2,1,0:T(8,128)(2,1)} %get-tuple-element.39.signs, ...), custom_call_target="tpu_custom_call" | custom-call | flops 20000000000 | bytes 10000000 | tf_op jit(solution)/shard_map/project2/pallas_call | solution.py:417
  286.6 2.8 multiply_convert_fusion
  289.5 0.8 slice.68
  290.4 0.7 slice.67
  291.3 4.1 mul.84
  295.4 7.0 %fusion.2 = f32[768,1024]{1,0:T(8,128)} fusion(bf16[768,1792]{1,0:T(8,128)(2,1)S(1)} %bitcast.89, bf16[3,1792,1024]{2,1,0:T(8,128)(2,1)} %means.5), kind=kOutput, calls=%fused_computation.2 | convolution fusion | flops 2818572288 | bytes 9568256 | tf_op jit(solution)/shard_map/dot_general | solution.py:22
  302.4 15.2 %grads2_0.1 = (bf16[3,1792,1024]{2,1,0:T(8,128)(2,1)}, bf16[3,1792,1024]{2,1,0:T(8,128)(2,1)}) custom-call(bf16[768,1792]{1,0:T(8,128)(2,1)} %bitcast.88, bf16[768,1792]{1,0:T(8,128)(2,1)} %bitcast.87, bf16[2,2,768,1024]{3,2,1,0:T(8,128)(2,1)} %bitcast.72, bf16[2,2,768,1024]{3,2,1,0:T(8,128)(2,1)} %bitcast.73, bf16[3,1792,1024]{2,1,0:T(8,128)(2,1)} %noise.7), custom_call_target="tpu_custom_call" | custom-call | flops 5637144576 | bytes 11010048 | tf_op jit(solution)/shard_map/grads2_0/pallas_call | solution.py:613
  317.6 6.2 %fusion.13 = bf16[768,1024]{1,0:T(8,128)(2,1)S(1)} fusion(f32[768,1024]{1,0:T(8,128)} %fusion.2, bf16[768,1792]{1,0:T(8,128)(2,1)S(1)} %bitcast.90, bf16[5376,1024]{1,0:T(8,128)(2,1)} %get-tuple-element.36, bf16[2,2,768,1024]{3,2,1,0:T(8,128)(2,1)} %bitcast.74), kind=kOutput, calls=%fused_computation.15 | convolution fusion | flops 2823290880 | bytes 12713984 | tf_op jit(solution)/shard_map/dot_general | solution.py:22
  323.8 21.3 %finish5.1 = bf16[24,4096]{1,0:T(8,128)(2,1)S(1)} custom-call(bf16[4,2,2,2,24,1024]{5,4,3,2,1,0:T(8,128)(2,1)S(1)} %bitcast.68), custom_call_target="tpu_custom_call" | custom-call | flops 10000000000 | bytes 10000000 | tf_op jit(solution)/shard_map/finish5/pallas_call | solution.py:560
  345.1 4.8 %all-gather.4.cloned.1.call-done.hid = bf16[768,1792]{1,0:T(8,128)(2,1)} async-done(((bf16[192,1792]{1,0:T(8,128)(2,1)}), bf16[768,1792]{1,0:T(8,128)(2,1)}) %all-gather.4.cloned.1.call-update) | async-done | bytes 2752528 | tf_op jit(solution)/shard_map/all_gather | solution.py:644
  349.9 7.6 %fusion = f32[768,1024]{1,0:T(8,128)} fusion(bf16[768,1792]{1,0:T(8,128)(2,1)} %all-gather.4.cloned.1.call-done.hid, bf16[3,1792,1024]{2,1,0:T(8,128)(2,1)} %means.5), kind=kOutput, calls=%fused_computation | convolution fusion | flops 2818572288 | bytes 9568256 | tf_op jit(solution)/shard_map/dot_general | solution.py:22
  357.6 6.9 %fusion.4 = f32[768,1024]{1,0:T(8,128)} fusion(bf16[5376,1024]{1,0:T(8,128)(2,1)} %get-tuple-element.36, bf16[768,1792]{1,0:T(8,128)(2,1)S(1)} %copy-done.10, bf16[768,1792]{1,0:T(8,128)(2,1)S(1)} %bitcast.92), kind=kOutput, calls=%fused_computation.4 | convolution fusion | flops 2819948544 | bytes 12320768 | tf_op jit(solution)/shard_map/dot_general | solution.py:22
  364.4 14.8 %grads1_0.1 = (bf16[3,1792,1024]{2,1,0:T(8,128)(2,1)}, bf16[3,1792,1024]{2,1,0:T(8,128)(2,1)}) custom-call(bf16[768,1792]{1,0:T(8,128)(2,1)} %all-gather.4.cloned.1.call-done.hid, bf16[768,1792]{1,0:T(8,128)(2,1)} %bitcast.91, bf16[2,2,768,1024]{3,2,1,0:T(8,128)(2,1)} %bitcast.75, ...), custom_call_target="tpu_custom_call", output_to_operand_aliasing={{0}: (5, {}), {1}: (6, {})} | custom-call | flops 5637144576 | bytes 11010048 | tf_op jit(solution)/shard_map/grads1_0/pallas_call | solution.py:613
  379.2 7.9 %all-gather.8.cloned.1.call-done.hid = bf16[768,1024]{1,0:T(8,128)(2,1)} async-done(((bf16[192,1024]{1,0:T(8,128)(2,1)}), bf16[768,1024]{1,0:T(8,128)(2,1)}) %all-gather.8.cloned.1.call-update) | async-done | bytes 1572880 | tf_op jit(solution)/shard_map/all_gather | solution.py:644
  387.1 9.8 %grads0_0.1 = (bf16[3,1792,1024]{2,1,0:T(8,128)(2,1)}, bf16[3,1792,1024]{2,1,0:T(8,128)(2,1)}) custom-call(bf16[768,1024]{1,0:T(8,128)(2,1)} %all-gather.8.cloned.1.call-done.hid, bf16[768,1792]{1,0:T(8,128)(2,1)} %bitcast.83, bf16[2,2,768,1024]{3,2,1,0:T(8,128)(2,1)} %bitcast.77, ...), custom_call_target="tpu_custom_call", output_to_operand_aliasing={{0}: (5, {}), {1}: (6, {})} | custom-call | flops 3221225472 | bytes 6291456 | tf_op jit(solution)/shard_map/grads0_0/pallas_call | solution.py:613
  396.9 6.6 %fusion.21 = f32[768,1024]{1,0:T(8,128)} fusion(f32[768,1024]{1,0:T(8,128)} %fusion, bf16[768,1024]{1,0:T(8,128)(2,1)} %all-gather.8.cloned.1.call-done.hid, bf16[3,1792,1024]{2,1,0:T(8,128)(2,1)} %means.5), kind=kOutput, calls=%fused_computation.22 | convolution fusion | flops 1611399168 | bytes 9961472 | tf_op jit(solution)/shard_map/dot_general | solution.py:22
  403.5 5.2 %fusion.24 = f32[768,1024]{1,0:T(8,128)} fusion(f32[768,1024]{1,0:T(8,128)S(1)} %copy-done.13, bf16[3,1792,1024]{2,1,0:T(8,128)(2,1)} %bitcast.97, bf16[768,1024]{1,0:T(8,128)(2,1)S(1)} %copy-done.11, bf16[768,1792]{1,0:T(8,128)(2,1)S(1)} %bitcast.85), kind=kOutput, calls=%fused_computation.23 | convolution fusion | flops 1612185600 | bytes 11534336 | tf_op jit(solution)/shard_map/dot_general | solution.py:22
  408.7 9.1 %all-gather.6.cloned.1.call-done.hid = bf16[768,768]{1,0:T(8,128)(2,1)} async-done(((bf16[192,768]{1,0:T(8,128)(2,1)}), bf16[768,768]{1,0:T(8,128)(2,1)}) %all-gather.6.cloned.1.call-update) | async-done | bytes 1179664 | tf_op jit(solution)/shard_map/all_gather | solution.py:644
  417.9 3.3 fusion.25
  421.2 0.7 copy-done.7
  421.9 3.6 fusion.11
  425.5 20.5 %finish6.1 = bf16[24,4096]{1,0:T(8,128)(2,1)S(1)} custom-call(bf16[4,2,2,2,24,1024]{5,4,3,2,1,0:T(8,128)(2,1)S(1)} %bitcast.67), custom_call_target="tpu_custom_call" | custom-call | flops 10000000000 | bytes 10000000 | tf_op jit(solution)/shard_map/finish6/pallas_call | solution.py:560
  446.0 8.2 %grads0_4.1 = (bf16[3,1792,1024]{2,1,0:T(8,128)(2,1)}, bf16[3,1792,1024]{2,1,0:T(8,128)(2,1)}) custom-call(bf16[768,768]{1,0:T(8,128)(2,1)} %all-gather.6.cloned.1.call-done.hid, bf16[768,1792]{1,0:T(8,128)(2,1)} %bitcast.84, bf16[2,2,768,1024]{3,2,1,0:T(8,128)(2,1)} %bitcast.80, ...), custom_call_target="tpu_custom_call", output_to_operand_aliasing={{0}: (5, {}), {1}: (6, {})} | custom-call | flops 2415919104 | bytes 4718592 | tf_op jit(solution)/shard_map/grads0_4/pallas_call | solution.py:613
  (36 shorter events, 2.4 us)
Async XLA Ops:
  7.2 342.7 %all-gather.4.cloned.1.call-start = ((), (), s32[]{:S(2)}) async-start(), calls=%async_computation | async-start | bytes 3440640 | tf_op jit(solution)/shard_map/all_gather | solution.py:644
  10.1 4.3 copy-start.12
  152.0 66.1 %copy-start.3 = (f32[192,1792]{1,0:T(8,128)S(1)}, f32[192,1792]{1,0:T(8,128)}, u32[]{:S(2)}) copy-start(f32[192,1792]{1,0:T(8,128)} %get-tuple-element.40) | copy-start | bytes 4128772
  220.6 66.0 %copy-start.4 = (f32[192,1792]{1,0:T(8,128)S(1)}, f32[192,1792]{1,0:T(8,128)}, u32[]{:S(2)}) copy-start(f32[192,1792]{1,0:T(8,128)} %get-tuple-element.41) | copy-start | bytes 4128772
  289.4 1.9 copy-start.1
  289.4 97.7 %all-gather.8.cloned.1.call-start = ((), (), s32[]{:S(2)}) async-start(), calls=%async_computation.2 | async-start | bytes 1966080 | tf_op jit(solution)/shard_map/all_gather | solution.py:644
  290.3 127.5 %all-gather.6.cloned.1.call-start = ((), (), s32[]{:S(2)}) async-start(), calls=%async_computation.1 | async-start | bytes 1474560 | tf_op jit(solution)/shard_map/all_gather | solution.py:644
  291.3 4.1 copy-start.2
  302.4 15.2 %copy-start.8 = (bf16[4,192,1792]{2,1,0:T(8,128)(2,1)S(1)}, bf16[4,192,1792]{2,1,0:T(8,128)(2,1)}, u32[]{:S(2)}) copy-start(bf16[4,192,1792]{2,1,0:T(8,128)(2,1)} %mul.84) | copy-start | bytes 8257540
  349.9 7.6 %copy-start.9 = (bf16[4,192,1792]{2,1,0:T(8,128)(2,1)S(1)}, bf16[4,192,1792]{2,1,0:T(8,128)(2,1)}, u32[]{:S(2)}) copy-start(bf16[4,192,1792]{2,1,0:T(8,128)(2,1)} %get-tuple-element.38.signs) | copy-start | bytes 8257540
  349.9 7.6 %copy-start.10 = (bf16[768,1792]{1,0:T(8,128)(2,1)S(1)}, bf16[768,1792]{1,0:T(8,128)(2,1)}, u32[]{:S(2)}) copy-start(bf16[768,1792]{1,0:T(8,128)(2,1)} %all-gather.4.cloned.1.call-done.hid) | copy-start | bytes 8257540
  396.9 6.6 %copy-start = (bf16[4,192,1792]{2,1,0:T(8,128)(2,1)S(1)}, bf16[4,192,1792]{2,1,0:T(8,128)(2,1)}, u32[]{:S(2)}) copy-start(bf16[4,192,1792]{2,1,0:T(8,128)(2,1)} %get-tuple-element.37.signs) | copy-start | bytes 8257540
  396.9 6.6 %copy-start.11 = (bf16[768,1024]{1,0:T(8,128)(2,1)S(1)}, bf16[768,1024]{1,0:T(8,128)(2,1)}, u32[]{:S(2)}) copy-start(bf16[768,1024]{1,0:T(8,128)(2,1)} %all-gather.8.cloned.1.call-done.hid) | copy-start | bytes 4718596
  396.9 6.6 %copy-start.13 = (f32[768,1024]{1,0:T(8,128)S(1)}, f32[768,1024]{1,0:T(8,128)}, u32[]{:S(2)}) copy-start(f32[768,1024]{1,0:T(8,128)} %fusion.4) | copy-start | bytes 9437188
  417.9 3.3 copy-start.5
  417.9 3.3 copy-start.6
  417.9 4.0 copy-start.7
Sparse Core Ops, SparseCore 0:
  289.6 60.3 all-gather.3
  351.5 35.6 all-gather.7
  388.7 29.1 all-gather.5

commit v3 on v2

--- a/solution.py
+++ b/solution.py
@@ -248,8 +248,9 @@
     _, _, _, rows, width = pairs.shape
     most = max(nx, ny)
     planes, hid, _ = sigma.shape
-    tile = 256 if hid % 256 == 0 else hid
     flat = (planes * hid, width)
+    fits = [t for t in range(16, 769, 16) if flat[0] % t == 0]
+    tile = max(fits) if fits else hid
     anywhere = pl.BlockSpec(memory_space=pl.ANY)
     within = pl.BlockSpec(memory_space=VMEM)
     bf16 = jnp.bfloat16
@@ -600,14 +601,15 @@
     sigma[...] = (total_pert * noise[...].astype(jnp.float32)).astype(jnp.bfloat16)
 
 
-def weight_grads(groups, k, half, scale, hid, sign, gathered, noise, into, begin=0):
-    tokens, ff = hid.shape
+def weight_grads(groups, k, half, scale, hid, sign, gathered, noise, into, span, at=0):
+    tokens = hid.shape[0]
+    ff = span.stop - span.start
     width = gathered.shape[3]
-    tile = 256 if ff % 256 == 0 and begin % 256 == 0 else ff
-    skip = begin // tile
+    tile = 256 if all(v % 256 == 0 for v in (ff, span.start, at)) else ff
+    skip, lead = span.start // tile, at // tile
     whole = lambda j: pl.BlockSpec((None, None, tokens, width), lambda i: (half, j, 0, 0))
     block = pl.BlockSpec((None, tile, width), lambda i: (k, skip + i, 0))
-    cols = pl.BlockSpec((tokens, tile), lambda i: (0, i))
+    cols = pl.BlockSpec((tokens, tile), lambda i: (0, lead + i))
     signs = pl.BlockSpec((tokens, tile), lambda i: (0, skip + i))
     keep = [pl.BlockSpec(memory_space=pl.ANY)] * len(into)
     return pl.pallas_call(
@@ -659,39 +661,41 @@
     gate_sig = jax.nn.sigmoid(gate)
     hidden = (gate * gate_sig * up).astype(bf16)
     hid_grad, hidden = project(4, 2, 1, scale_out, gathered, weight_means, perturb, s2, hidden)
-    up_grad = share((hid_grad * gate * gate_sig).astype(bf16))
+    up_grad = (hid_grad * gate * gate_sig).astype(bf16)
     gate_grad = (hid_grad * up * gate_sig * (1.0 + gate * (1.0 - gate_sig))).astype(bf16)
     ff = gate_grad.shape[1]
-    cut = -(-ff // 512) * 256 if ff % 256 == 0 else ff
-    spans = [slice(0, cut), slice(cut, ff)] if cut < ff else [slice(0, ff)]
-    gate_grads = [share(gate_grad[:, span]) for span in spans]
+    lead = ff // 256 * 2 // 7 * 256 if ff % 256 == 0 else 0
+    early = share(jnp.concatenate([up_grad, gate_grad[:, :lead]], axis=1))
+    late = share(gate_grad[:, lead:])
     hidden, s0, s1, s2 = (v.reshape(-1, v.shape[2]) for v in (hidden, s0, s1, s2))
 
-    def back(k, value, sign, span=slice(None)):
+    def back(k, value, sign, span):
         return (
             dot(value, weight_means[k, span], ((1,), (0,))),
             dot(value * sign[:, span], perturb[k, span], ((1,), (0,))),
         )
 
-    mean, pert = back(2, hidden, s2)
+    def grads_of(k, half, scale, value, sign, into, span, at=0):
+        return weight_grads(
+            groups, k, half, scale, value, sign, gathered, weight_noise, into, span, at
+        )
+
+    every, head, tail = slice(0, ff), slice(0, lead), slice(lead, ff)
+    mean, pert = back(2, hidden, s2, every)
     result = finish(5, (scale_out * mean + scale_out * pert * r.astype(f32)).astype(bf16))
-    grads = weight_grads(groups, 2, 1, scale_out, hidden, s2, gathered, weight_noise, ())
-    up_grad, result, *grads = lax.optimization_barrier((up_grad, result, *grads))
-    up_mean, up_pert = back(1, up_grad, s1)
-    grads = weight_grads(groups, 1, 0, scale_in, up_grad, s1, gathered, weight_noise, grads)
-    mean, pert = up_mean, up_pert
-    for span, value in zip(spans, gate_grads):
-        value, mean, pert, *grads = lax.optimization_barrier((value, mean, pert, *grads))
-        gate_mean, gate_pert = back(0, value, s0, span)
+    grads = grads_of(2, 1, scale_out, hidden, s2, (), every)
+    early, result, *grads = lax.optimization_barrier((early, result, *grads))
+    mean, pert = back(1, early[:, :ff], s1, every)
+    grads = grads_of(1, 0, scale_in, early, s1, grads, every)
+    if lead:
+        gate_mean, gate_pert = back(0, early[:, ff:], s0, head)
         mean, pert = mean + gate_mean, pert + gate_pert
-        if span.stop == ff:
-            input_grad = finish(
-                6, (scale_in * mean + scale_in * pert * a.astype(f32)).astype(bf16)
-            )
-        grads = weight_grads(
-            groups, 0, 0, scale_in, value, s0, gathered, weight_noise, grads, span.start
-        )
-    mean_grad, sigma_grad = grads
+        grads = grads_of(0, 0, scale_in, early, s0, grads, head, ff)
+    late, mean, pert, *grads = lax.optimization_barrier((late, mean, pert, *grads))
+    gate_mean, gate_pert = back(0, late, s0, tail)
+    mean, pert = mean + gate_mean, pert + gate_pert
+    input_grad = finish(6, (scale_in * mean + scale_in * pert * a.astype(f32)).astype(bf16))
+    mean_grad, sigma_grad = grads_of(0, 0, scale_in, late, s0, grads, tail)
     return (result, input_grad, mean_grad, sigma_grad)
 
 

time: 463 us -> 456 us (0.985)
  matrix products: 46.4 us -> 41.7 us
    dot_general x8, matrix products: 46.4 us -> 41.7 us  [dot(): lax.dot_general(left, right, (dims, ((), ())), preferred_element_type=jnp...]
    all_gather x3 -> x2, waiting for transfers between devices: 21.8 us -> 21.2 us  [share(): return lax.all_gather(value, 'dp', axis=0, tiled=True)]
  transfers between devices with their start and end apart: 3 -> 2, of which waited for: 3 -> 2; matrix products, arithmetic and copies ran while one was open for 10% -> 8% of each run, Pallas kernels for 13% -> 13%
where the time goes in v3:
time: 456 us
  Pallas kernels  358 us (79%)
  matrix products  41.7 us (9%)
  waiting for transfers between devices  21.3 us (5%)
  other arithmetic  16.2 us (4%)
  between operations  14.2 us (3%)
    pallas_call x3, Pallas kernels, project(): pl.pallas_call(functools.partial(project_kernel, scale, k, half), out_sha...  196 us
    pallas_call x1, Pallas kernels, spread(): pl.pallas_call(spread_kernel, out_shape=[jax.ShapeDtypeStruct((2, 2, nz,...  71.9 us
    pallas_call x4, Pallas kernels, weight_grads(): pl.pallas_call(functools.partial(grad_kernel, groups, scale), grid=(ff //...  47.8 us
    pallas_call x2, Pallas kernels, finish(): pl.pallas_call(finish_kernel, out_shape=jax.ShapeDtypeStruct((rows, nz *...  41.9 us
    dot_general x8, matrix products, dot(): lax.dot_general(left, right, (dims, ((), ())), preferred_element_type=jnp...  41.7 us
    all_gather x2, waiting for transfers between devices, share(): return lax.all_gather(value, 'dp', axis=0, tiled=True)  21.2 us
  transfers between devices with their start and end apart: 2, of which 2 were waited for; matrix products, arithmetic and copies ran while one was open for 8% of the time, Pallas kernels for 13%

profile of v3, /device:TPU:0, one launch (start us, length us, event | category | flops | bytes accessed | tf_op | source)
XLA Modules:
  0.0 455.7 jit_solution(14624253516511381798)
XLA Ops:
  7.2 1.2 fusion.32
  8.4 1.1 pad_maximum_fusion.1
  10.1 1.1 copy.21
  11.3 3.1 fusion.30
  14.4 1.0 fusion.31.shard
  15.4 71.9 %spread.1 = (bf16[2,2,4,2,2,2,24,1024]{7,6,5,4,3,2,1,0:T(8,128)(2,1)}, bf16[5376,1024]{1,0:T(8,128)(2,1)}, bf16[4,192,1792]{2,1,0:T(8,128)(2,1)}) custom-call(bf16[2,2,4,24,1024]{4,3,2,1,0:T(8,128)(2,1)} %bitcast.89, bf16[5376,1024]{1,0:T(8,128)(2,1)} %bitcast.97, bf16[5376,1024]{1,0:T(8,128)(2,1)} %bitcast.78, bf16[192,1792]{1,0:T(8,128)(2,1)} %get-tuple-element.59.shard), custom_call_target="tpu_custom_call" | custom-call | flops 10000000000 | bytes 10000000 | tf_op jit(solution)/shard_map/spread/pallas_call | solution.py:257
  87.3 64.6 %project0.1 = (f32[192,1792]{1,0:T(8,128)}, bf16[4,192,1792]{2,1,0:T(8,128)(2,1)}) custom-call(bf16[2,2,768,1024]{3,2,1,0:T(8,128)(2,1)} %bitcast.65, bf16[3,1792,1024]{2,1,0:T(8,128)(2,1)} %means.5, bf16[3,1792,1024]{2,1,0:T(8,128)(2,1)} %bitcast.92, bf16[4,192,1792]{2,1,0:T(8,128)(2,1)} %get-tuple-element.32.signs, bf16[192,1792]{1,0:T(8,128)(2,1)} %get-tuple-element.58.shard), custom_call_target="tpu_custom_call" | custom-call | flops 20000000000 | bytes 10000000 | tf_op jit(solution)/shard_map/project0/pallas_call | solution.py:418
  151.9 66.0 %project1.1 = (f32[192,1792]{1,0:T(8,128)}, bf16[4,192,1792]{2,1,0:T(8,128)(2,1)}) custom-call(bf16[2,2,768,1024]{3,2,1,0:T(8,128)(2,1)} %bitcast.66, bf16[3,1792,1024]{2,1,0:T(8,128)(2,1)} %means.5, bf16[3,1792,1024]{2,1,0:T(8,128)(2,1)} %bitcast.93, bf16[4,192,1792]{2,1,0:T(8,128)(2,1)} %get-tuple-element.33.signs, bf16[192,1792]{1,0:T(8,128)(2,1)} %fusion.31.shard), custom_call_target="tpu_custom_call" | custom-call | flops 20000000000 | bytes 10000000 | tf_op jit(solution)/shard_map/project1/pallas_call | solution.py:418
  218.0 2.6 multiply_convert_fusion.2.shard
  220.5 65.8 %project2.1 = (f32[192,1792]{1,0:T(8,128)}, bf16[4,192,1792]{2,1,0:T(8,128)(2,1)}) custom-call(bf16[2,2,768,1024]{3,2,1,0:T(8,128)(2,1)} %bitcast.67, bf16[3,1792,1024]{2,1,0:T(8,128)(2,1)} %means.5, bf16[3,1792,1024]{2,1,0:T(8,128)(2,1)} %bitcast.94, bf16[4,192,1792]{2,1,0:T(8,128)(2,1)} %get-tuple-element.34.signs, ...), custom_call_target="tpu_custom_call" | custom-call | flops 20000000000 | bytes 10000000 | tf_op jit(solution)/shard_map/project2/pallas_call | solution.py:418
  286.4 2.0 multiply_convert_fusion.1
  288.4 1.0 pad_maximum_fusion
  289.6 0.8 slice.76
  290.5 4.1 mul.88
  294.7 7.1 %fusion.2 = f32[768,1024]{1,0:T(8,128)} fusion(bf16[768,1792]{1,0:T(8,128)(2,1)S(1)} %bitcast.85, bf16[3,1792,1024]{2,1,0:T(8,128)(2,1)} %means.5), kind=kOutput, calls=%fused_computation.2 | convolution fusion | flops 2818572288 | bytes 9568256 | tf_op jit(solution)/shard_map/dot_general | solution.py:22
  301.7 15.0 %grads2_0.1 = (bf16[3,1792,1024]{2,1,0:T(8,128)(2,1)}, bf16[3,1792,1024]{2,1,0:T(8,128)(2,1)}) custom-call(bf16[768,1792]{1,0:T(8,128)(2,1)} %bitcast.84, bf16[768,1792]{1,0:T(8,128)(2,1)} %bitcast.83, bf16[2,2,768,1024]{3,2,1,0:T(8,128)(2,1)} %bitcast.68, bf16[2,2,768,1024]{3,2,1,0:T(8,128)(2,1)} %bitcast.69, bf16[3,1792,1024]{2,1,0:T(8,128)(2,1)} %noise.7), custom_call_target="tpu_custom_call" | custom-call | flops 5637144576 | bytes 11010048 | tf_op jit(solution)/shard_map/grads2_0/pallas_call | solution.py:615
  316.8 6.2 %fusion.13 = bf16[768,1024]{1,0:T(8,128)(2,1)S(1)} fusion(f32[768,1024]{1,0:T(8,128)} %fusion.2, bf16[768,1792]{1,0:T(8,128)(2,1)S(1)} %bitcast.86, bf16[5376,1024]{1,0:T(8,128)(2,1)} %get-tuple-element.31, bf16[2,2,768,1024]{3,2,1,0:T(8,128)(2,1)} %bitcast.70), kind=kOutput, calls=%fused_computation.15 | convolution fusion | flops 2823290880 | bytes 12713984 | tf_op jit(solution)/shard_map/dot_general | solution.py:22
  323.0 21.3 %finish5.1 = bf16[24,4096]{1,0:T(8,128)(2,1)S(1)} custom-call(bf16[4,2,2,2,24,1024]{5,4,3,2,1,0:T(8,128)(2,1)S(1)} %bitcast.64), custom_call_target="tpu_custom_call" | custom-call | flops 10000000000 | bytes 10000000 | tf_op jit(solution)/shard_map/finish5/pallas_call | solution.py:561
  344.3 18.1 %all-gather.3.cloned.1.call-done.hid = bf16[768,2304]{1,0:T(8,128)(2,1)} async-done(((bf16[192,2304]{1,0:T(8,128)(2,1)}), bf16[768,2304]{1,0:T(8,128)(2,1)}) %all-gather.3.cloned.1.call-update) | async-done | bytes 3538960 | tf_op jit(solution)/shard_map/all_gather | solution.py:646
  362.4 14.7 %grads1_0.1 = (bf16[3,1792,1024]{2,1,0:T(8,128)(2,1)}, bf16[3,1792,1024]{2,1,0:T(8,128)(2,1)}) custom-call(bf16[768,2304]{1,0:T(8,128)(2,1)} %all-gather.3.cloned.1.call-done.hid, bf16[768,1792]{1,0:T(8,128)(2,1)} %bitcast.87, bf16[2,2,768,1024]{3,2,1,0:T(8,128)(2,1)} %bitcast.71, ...), custom_call_target="tpu_custom_call", output_to_operand_aliasing={{0}: (5, {}), {1}: (6, {})} | custom-call | flops 5637144576 | bytes 11010048 | tf_op jit(solution)/shard_map/grads1_0/pallas_call | solution.py:615
  377.1 6.6 %grads0_0.1 = (bf16[3,1792,1024]{2,1,0:T(8,128)(2,1)}, bf16[3,1792,1024]{2,1,0:T(8,128)(2,1)}) custom-call(bf16[768,2304]{1,0:T(8,128)(2,1)} %all-gather.3.cloned.1.call-done.hid, bf16[768,1792]{1,0:T(8,128)(2,1)} %bitcast.79, bf16[2,2,768,1024]{3,2,1,0:T(8,128)(2,1)} %bitcast.73, ...), custom_call_target="tpu_custom_call", output_to_operand_aliasing={{0}: (5, {}), {1}: (6, {})} | custom-call | flops 1610612736 | bytes 3145728 | tf_op jit(solution)/shard_map/grads0_0/pallas_call | solution.py:615
  383.7 6.0 %fusion = f32[768,1024]{1,0:T(8,128)S(1)} fusion(bf16[3,1792,1024]{2,1,0:T(8,128)(2,1)} %means.5, bf16[768,2304]{1,0:T(8,128)(2,1)} %all-gather.3.cloned.1.call-done.hid), kind=kOutput, calls=%fused_computation | convolution fusion | flops 2818572288 | bytes 9568256 | tf_op jit(solution)/shard_map/dot_general | solution.py:22
  389.8 4.0 convolution_add_fusion.1
  393.7 5.2 %fusion.4 = f32[768,1024]{1,0:T(8,128)S(1)} fusion(bf16[5376,1024]{1,0:T(8,128)(2,1)} %get-tuple-element.31, bf16[768,1792]{1,0:T(8,128)(2,1)S(1)} %bitcast.88, bf16[768,2304]{1,0:T(8,128)(2,1)S(1)} %copy-done), kind=kOutput, calls=%fused_computation.4 | convolution fusion | flops 2819948544 | bytes 12320768 | tf_op jit(solution)/shard_map/dot_general | solution.py:22
  399.0 3.9 convolution_add_fusion
  402.8 3.2 all-gather.5.cloned.1.call-done.hid
  406.0 4.7 %fusion.15 = f32[768,1024]{1,0:T(8,128)S(1)} fusion(bf16[3,1792,1024]{2,1,0:T(8,128)(2,1)} %bitcast.96, bf16[768,1280]{1,0:T(8,128)(2,1)} %all-gather.5.cloned.1.call-done.hid, bf16[768,1792]{1,0:T(8,128)(2,1)S(1)} %bitcast.82), kind=kOutput, calls=%fused_computation.18 | convolution fusion | flops 2014248960 | bytes 9699328 | tf_op jit(solution)/shard_map/dot_general | solution.py:22
  410.8 4.6 %fusion.11 = bf16[768,1024]{1,0:T(8,128)(2,1)S(1)} fusion(f32[768,1024]{1,0:T(8,128)S(1)} %copy-done.6, f32[768,1024]{1,0:T(8,128)S(1)} %fusion.15, f32[768,1024]{1,0:T(8,128)S(1)} %copy-done.7, bf16[2,2,768,1024]{3,2,1,0:T(8,128)(2,1)} %bitcast.75, bf16[768,1280]{1,0:T(8,128)(2,1)S(1)} %copy-done.10, bf16[3,1792,1024]{2,1,0:T(8,128)(2,1)} %means.5), kind=kOutput, calls=%fused_computation.12 | convolution fusion | flops 2019557376 | bytes 17170432 | tf_op jit(solution)/shard_map/dot_general | solution.py:22
  415.4 20.5 %finish6.1 = bf16[24,4096]{1,0:T(8,128)(2,1)S(1)} custom-call(bf16[4,2,2,2,24,1024]{5,4,3,2,1,0:T(8,128)(2,1)S(1)} %bitcast.63), custom_call_target="tpu_custom_call" | custom-call | flops 10000000000 | bytes 10000000 | tf_op jit(solution)/shard_map/finish6/pallas_call | solution.py:561
  436.0 11.5 %grads0_2.1 = (bf16[3,1792,1024]{2,1,0:T(8,128)(2,1)}, bf16[3,1792,1024]{2,1,0:T(8,128)(2,1)}) custom-call(bf16[768,1280]{1,0:T(8,128)(2,1)} %all-gather.5.cloned.1.call-done.hid, bf16[768,1792]{1,0:T(8,128)(2,1)} %bitcast.80, bf16[2,2,768,1024]{3,2,1,0:T(8,128)(2,1)} %bitcast.76, ...), custom_call_target="tpu_custom_call", output_to_operand_aliasing={{0}: (5, {}), {1}: (6, {})} | custom-call | flops 4026531840 | bytes 7864320 | tf_op jit(solution)/shard_map/grads0_2/pallas_call | solution.py:615
  447.5 0.7 copy.30
  448.2 0.7 copy.31
  (30 shorter events, 1.0 us)
Async XLA Ops:
  7.2 355.2 %all-gather.3.cloned.1.call-start = ((), (), s32[]{:S(2)}) async-start(), calls=%async_computation | async-start | bytes 4423680 | tf_op jit(solution)/shard_map/all_gather | solution.py:646
  10.1 4.3 copy-start.11
  151.9 66.0 %copy-start.4 = (f32[192,1792]{1,0:T(8,128)S(1)}, f32[192,1792]{1,0:T(8,128)}, u32[]{:S(2)}) copy-start(f32[192,1792]{1,0:T(8,128)} %get-tuple-element.35) | copy-start | bytes 4128772
  220.5 65.8 %copy-start.5 = (f32[192,1792]{1,0:T(8,128)S(1)}, f32[192,1792]{1,0:T(8,128)}, u32[]{:S(2)}) copy-start(f32[192,1792]{1,0:T(8,128)} %get-tuple-element.36) | copy-start | bytes 4128772
  288.4 2.1 copy-start.2
  289.4 116.6 %all-gather.5.cloned.1.call-start = ((), (), s32[]{:S(2)}) async-start(), calls=%async_computation.1 | async-start | bytes 2457600 | tf_op jit(solution)/shard_map/all_gather | solution.py:646
  290.5 4.2 copy-start.3
  301.7 15.0 %copy-start.8 = (bf16[4,192,1792]{2,1,0:T(8,128)(2,1)S(1)}, bf16[4,192,1792]{2,1,0:T(8,128)(2,1)}, u32[]{:S(2)}) copy-start(bf16[4,192,1792]{2,1,0:T(8,128)(2,1)} %mul.88) | copy-start | bytes 8257540
  383.7 6.0 %copy-start = (bf16[768,2304]{1,0:T(8,128)(2,1)S(1)}, bf16[768,2304]{1,0:T(8,128)(2,1)}, u32[]{:S(2)}) copy-start(bf16[768,2304]{1,0:T(8,128)(2,1)} %all-gather.3.cloned.1.call-done.hid) | copy-start | bytes 10616836
  389.7 4.0 copy-start.9
  393.7 5.2 %copy-start.1 = (bf16[4,192,1792]{2,1,0:T(8,128)(2,1)S(1)}, bf16[4,192,1792]{2,1,0:T(8,128)(2,1)}, u32[]{:S(2)}) copy-start(bf16[4,192,1792]{2,1,0:T(8,128)(2,1)} %get-tuple-element.32.signs) | copy-start | bytes 8257540
  406.0 4.7 %copy-start.6 = (f32[768,1024]{1,0:T(8,128)S(1)}, f32[768,1024]{1,0:T(8,128)}, u32[]{:S(2)}) copy-start(f32[768,1024]{1,0:T(8,128)} %convolution_add_fusion) | copy-start | bytes 9437188
  406.0 4.7 %copy-start.7 = (f32[768,1024]{1,0:T(8,128)S(1)}, f32[768,1024]{1,0:T(8,128)}, u32[]{:S(2)}) copy-start(f32[768,1024]{1,0:T(8,128)} %convolution_add_fusion.1) | copy-start | bytes 9437188
  406.0 4.8 %copy-start.10 = (bf16[768,1280]{1,0:T(8,128)(2,1)S(1)}, bf16[768,1280]{1,0:T(8,128)(2,1)}, u32[]{:S(2)}) copy-start(bf16[768,1280]{1,0:T(8,128)(2,1)} %all-gather.5.cloned.1.call-done.hid) | copy-start | bytes 5898244
Sparse Core Ops, SparseCore 0:
  289.5 72.8 all-gather.2
  364.0 41.9 all-gather.4

commit v4 on v3

--- a/solution.py
+++ b/solution.py
@@ -158,6 +158,7 @@
         sends.append(copy)
         return copy
 
+    line.begin()
     local = []
     for p in range(2):
         keep = pltpu.make_async_copy(src.at[p, :, z], out.at[p, :, z, y, x, c], own.at[p])
@@ -215,20 +216,19 @@
     a, b, last = {}, {}, []
     for p in range(2):
         a[p, 0] = first(p, 0)
-    line.begin()
     perturb_tiles(sigma, noise, perturb, wide, made, load, store)
+    line.relay(1)
     for k in range(1, nz):
         for p in range(2):
             a[p, k] = first(p, k)
     for p in range(2):
         b[p, 0] = second(p, 0, a[p, 0])
-    line.relay(1)
+    line.relay(2)
     for k in range(1, nz):
         for p in range(2):
             b[p, k] = second(p, k, a[p, k])
     for p in range(2):
         last += third(p, 0, b[p, 0])
-    line.relay(2)
     for k in range(1, nz):
         for p in range(2):
             last += third(p, k, b[p, k])

time: 456 us -> 462 us (1.013)
  Pallas kernels: 358 us -> 365 us
    pallas_call x3, Pallas kernels: 196 us -> 204 us  [project(): pl.pallas_call(functools.partial(project_kernel, scale, k, half), out_sha...]
  transfers between devices with their start and end apart: 2 -> 2, of which waited for: 2 -> 2; matrix products, arithmetic and copies ran while one was open for 8% -> 8% of each run, Pallas kernels for 13% -> 12%
where the time goes in v4:
time: 462 us; the launch traced here: 461 us
  Pallas kernels  365 us (79%)
  matrix products  41.5 us (9%)
  waiting for transfers between devices  20.4 us (4%)
  other arithmetic  16.2 us (4%)
  between operations  14.2 us (3%)
    pallas_call x3, Pallas kernels, project(): pl.pallas_call(functools.partial(project_kernel, scale, k, half), out_sha...  204 us
    pallas_call x1, Pallas kernels, spread(): pl.pallas_call(spread_kernel, out_shape=[jax.ShapeDtypeStruct((2, 2, nz,...  71.8 us
    pallas_call x4, Pallas kernels, weight_grads(): pl.pallas_call(functools.partial(grad_kernel, groups, scale), grid=(ff //...  47.8 us
    pallas_call x2, Pallas kernels, finish(): pl.pallas_call(finish_kernel, out_shape=jax.ShapeDtypeStruct((rows, nz *...  41.6 us
    dot_general x8, matrix products, dot(): lax.dot_general(left, right, (dims, ((), ())), preferred_element_type=jnp...  41.5 us
    all_gather x2, waiting for transfers between devices, share(): return lax.all_gather(value, 'dp', axis=0, tiled=True)  20.4 us
  transfers between devices with their start and end apart: 2, of which 2 were waited for; matrix products, arithmetic and copies ran while one was open for 8% of the time, Pallas kernels for 12%

profile of v4, /device:TPU:0, one launch (start us, length us, event | category | flops | bytes accessed | tf_op | source)
XLA Modules:
  0.0 461.5 jit_solution(17042642288172085039)
XLA Ops:
  7.2 1.2 fusion.32
  8.4 1.1 pad_maximum_fusion.1
  10.1 1.1 copy.21
  11.3 3.1 fusion.30
  14.4 1.0 fusion.31.shard
  15.4 71.8 %spread.1 = (bf16[2,2,4,2,2,2,24,1024]{7,6,5,4,3,2,1,0:T(8,128)(2,1)}, bf16[5376,1024]{1,0:T(8,128)(2,1)}, bf16[4,192,1792]{2,1,0:T(8,128)(2,1)}) custom-call(bf16[2,2,4,24,1024]{4,3,2,1,0:T(8,128)(2,1)} %bitcast.89, bf16[5376,1024]{1,0:T(8,128)(2,1)} %bitcast.97, bf16[5376,1024]{1,0:T(8,128)(2,1)} %bitcast.78, bf16[192,1792]{1,0:T(8,128)(2,1)} %get-tuple-element.59.shard), custom_call_target="tpu_custom_call" | custom-call | flops 10000000000 | bytes 10000000 | tf_op jit(solution)/shard_map/spread/pallas_call | solution.py:257
  87.2 72.2 %project0.1 = (f32[192,1792]{1,0:T(8,128)}, bf16[4,192,1792]{2,1,0:T(8,128)(2,1)}) custom-call(bf16[2,2,768,1024]{3,2,1,0:T(8,128)(2,1)} %bitcast.65, bf16[3,1792,1024]{2,1,0:T(8,128)(2,1)} %means.5, bf16[3,1792,1024]{2,1,0:T(8,128)(2,1)} %bitcast.92, bf16[4,192,1792]{2,1,0:T(8,128)(2,1)} %get-tuple-element.32.signs, bf16[192,1792]{1,0:T(8,128)(2,1)} %get-tuple-element.58.shard), custom_call_target="tpu_custom_call" | custom-call | flops 20000000000 | bytes 10000000 | tf_op jit(solution)/shard_map/project0/pallas_call | solution.py:418
  159.4 66.8 %project1.1 = (f32[192,1792]{1,0:T(8,128)}, bf16[4,192,1792]{2,1,0:T(8,128)(2,1)}) custom-call(bf16[2,2,768,1024]{3,2,1,0:T(8,128)(2,1)} %bitcast.66, bf16[3,1792,1024]{2,1,0:T(8,128)(2,1)} %means.5, bf16[3,1792,1024]{2,1,0:T(8,128)(2,1)} %bitcast.93, bf16[4,192,1792]{2,1,0:T(8,128)(2,1)} %get-tuple-element.33.signs, bf16[192,1792]{1,0:T(8,128)(2,1)} %fusion.31.shard), custom_call_target="tpu_custom_call" | custom-call | flops 20000000000 | bytes 10000000 | tf_op jit(solution)/shard_map/project1/pallas_call | solution.py:418
  226.2 2.6 multiply_convert_fusion.2.shard
  228.8 64.6 %project2.1 = (f32[192,1792]{1,0:T(8,128)}, bf16[4,192,1792]{2,1,0:T(8,128)(2,1)}) custom-call(bf16[2,2,768,1024]{3,2,1,0:T(8,128)(2,1)} %bitcast.67, bf16[3,1792,1024]{2,1,0:T(8,128)(2,1)} %means.5, bf16[3,1792,1024]{2,1,0:T(8,128)(2,1)} %bitcast.94, bf16[4,192,1792]{2,1,0:T(8,128)(2,1)} %get-tuple-element.34.signs, ...), custom_call_target="tpu_custom_call" | custom-call | flops 20000000000 | bytes 10000000 | tf_op jit(solution)/shard_map/project2/pallas_call | solution.py:418
  293.5 2.0 multiply_convert_fusion.1
  295.5 1.0 pad_maximum_fusion
  296.7 0.8 slice.76
  297.6 4.1 mul.88
  301.8 6.9 %fusion.2 = f32[768,1024]{1,0:T(8,128)} fusion(bf16[768,1792]{1,0:T(8,128)(2,1)S(1)} %bitcast.85, bf16[3,1792,1024]{2,1,0:T(8,128)(2,1)} %means.5), kind=kOutput, calls=%fused_computation.2 | convolution fusion | flops 2818572288 | bytes 9568256 | tf_op jit(solution)/shard_map/dot_general | solution.py:22
  308.7 15.0 %grads2_0.1 = (bf16[3,1792,1024]{2,1,0:T(8,128)(2,1)}, bf16[3,1792,1024]{2,1,0:T(8,128)(2,1)}) custom-call(bf16[768,1792]{1,0:T(8,128)(2,1)} %bitcast.84, bf16[768,1792]{1,0:T(8,128)(2,1)} %bitcast.83, bf16[2,2,768,1024]{3,2,1,0:T(8,128)(2,1)} %bitcast.68, bf16[2,2,768,1024]{3,2,1,0:T(8,128)(2,1)} %bitcast.69, bf16[3,1792,1024]{2,1,0:T(8,128)(2,1)} %noise.7), custom_call_target="tpu_custom_call" | custom-call | flops 5637144576 | bytes 11010048 | tf_op jit(solution)/shard_map/grads2_0/pallas_call | solution.py:615
  323.7 6.2 %fusion.13 = bf16[768,1024]{1,0:T(8,128)(2,1)S(1)} fusion(f32[768,1024]{1,0:T(8,128)} %fusion.2, bf16[768,1792]{1,0:T(8,128)(2,1)S(1)} %bitcast.86, bf16[5376,1024]{1,0:T(8,128)(2,1)} %get-tuple-element.31, bf16[2,2,768,1024]{3,2,1,0:T(8,128)(2,1)} %bitcast.70), kind=kOutput, calls=%fused_computation.15 | convolution fusion | flops 2823290880 | bytes 12713984 | tf_op jit(solution)/shard_map/dot_general | solution.py:22
  329.9 21.0 %finish5.1 = bf16[24,4096]{1,0:T(8,128)(2,1)S(1)} custom-call(bf16[4,2,2,2,24,1024]{5,4,3,2,1,0:T(8,128)(2,1)S(1)} %bitcast.64), custom_call_target="tpu_custom_call" | custom-call | flops 10000000000 | bytes 10000000 | tf_op jit(solution)/shard_map/finish5/pallas_call | solution.py:561
  351.0 17.2 %all-gather.3.cloned.1.call-done.hid = bf16[768,2304]{1,0:T(8,128)(2,1)} async-done(((bf16[192,2304]{1,0:T(8,128)(2,1)}), bf16[768,2304]{1,0:T(8,128)(2,1)}) %all-gather.3.cloned.1.call-update) | async-done | bytes 3538960 | tf_op jit(solution)/shard_map/all_gather | solution.py:646
  368.2 14.7 %grads1_0.1 = (bf16[3,1792,1024]{2,1,0:T(8,128)(2,1)}, bf16[3,1792,1024]{2,1,0:T(8,128)(2,1)}) custom-call(bf16[768,2304]{1,0:T(8,128)(2,1)} %all-gather.3.cloned.1.call-done.hid, bf16[768,1792]{1,0:T(8,128)(2,1)} %bitcast.87, bf16[2,2,768,1024]{3,2,1,0:T(8,128)(2,1)} %bitcast.71, ...), custom_call_target="tpu_custom_call", output_to_operand_aliasing={{0}: (5, {}), {1}: (6, {})} | custom-call | flops 5637144576 | bytes 11010048 | tf_op jit(solution)/shard_map/grads1_0/pallas_call | solution.py:615
  382.9 6.6 %grads0_0.1 = (bf16[3,1792,1024]{2,1,0:T(8,128)(2,1)}, bf16[3,1792,1024]{2,1,0:T(8,128)(2,1)}) custom-call(bf16[768,2304]{1,0:T(8,128)(2,1)} %all-gather.3.cloned.1.call-done.hid, bf16[768,1792]{1,0:T(8,128)(2,1)} %bitcast.79, bf16[2,2,768,1024]{3,2,1,0:T(8,128)(2,1)} %bitcast.73, ...), custom_call_target="tpu_custom_call", output_to_operand_aliasing={{0}: (5, {}), {1}: (6, {})} | custom-call | flops 1610612736 | bytes 3145728 | tf_op jit(solution)/shard_map/grads0_0/pallas_call | solution.py:615
  389.5 6.0 %fusion = f32[768,1024]{1,0:T(8,128)S(1)} fusion(bf16[3,1792,1024]{2,1,0:T(8,128)(2,1)} %means.5, bf16[768,2304]{1,0:T(8,128)(2,1)} %all-gather.3.cloned.1.call-done.hid), kind=kOutput, calls=%fused_computation | convolution fusion | flops 2818572288 | bytes 9568256 | tf_op jit(solution)/shard_map/dot_general | solution.py:22
  395.6 4.0 convolution_add_fusion.1
  399.5 5.2 %fusion.4 = f32[768,1024]{1,0:T(8,128)S(1)} fusion(bf16[5376,1024]{1,0:T(8,128)(2,1)} %get-tuple-element.31, bf16[768,1792]{1,0:T(8,128)(2,1)S(1)} %bitcast.88, bf16[768,2304]{1,0:T(8,128)(2,1)S(1)} %copy-done), kind=kOutput, calls=%fused_computation.4 | convolution fusion | flops 2819948544 | bytes 12320768 | tf_op jit(solution)/shard_map/dot_general | solution.py:22
  404.8 3.9 convolution_add_fusion
  408.7 3.2 all-gather.5.cloned.1.call-done.hid
  411.8 4.7 %fusion.15 = f32[768,1024]{1,0:T(8,128)S(1)} fusion(bf16[3,1792,1024]{2,1,0:T(8,128)(2,1)} %bitcast.96, bf16[768,1280]{1,0:T(8,128)(2,1)} %all-gather.5.cloned.1.call-done.hid, bf16[768,1792]{1,0:T(8,128)(2,1)S(1)} %bitcast.82), kind=kOutput, calls=%fused_computation.18 | convolution fusion | flops 2014248960 | bytes 9699328 | tf_op jit(solution)/shard_map/dot_general | solution.py:22
  416.6 4.6 %fusion.11 = bf16[768,1024]{1,0:T(8,128)(2,1)S(1)} fusion(f32[768,1024]{1,0:T(8,128)S(1)} %copy-done.6, f32[768,1024]{1,0:T(8,128)S(1)} %fusion.15, f32[768,1024]{1,0:T(8,128)S(1)} %copy-done.7, bf16[2,2,768,1024]{3,2,1,0:T(8,128)(2,1)} %bitcast.75, bf16[768,1280]{1,0:T(8,128)(2,1)S(1)} %copy-done.10, bf16[3,1792,1024]{2,1,0:T(8,128)(2,1)} %means.5), kind=kOutput, calls=%fused_computation.12 | convolution fusion | flops 2019557376 | bytes 17170432 | tf_op jit(solution)/shard_map/dot_general | solution.py:22
  421.2 20.5 %finish6.1 = bf16[24,4096]{1,0:T(8,128)(2,1)S(1)} custom-call(bf16[4,2,2,2,24,1024]{5,4,3,2,1,0:T(8,128)(2,1)S(1)} %bitcast.63), custom_call_target="tpu_custom_call" | custom-call | flops 10000000000 | bytes 10000000 | tf_op jit(solution)/shard_map/finish6/pallas_call | solution.py:561
  441.8 11.5 %grads0_2.1 = (bf16[3,1792,1024]{2,1,0:T(8,128)(2,1)}, bf16[3,1792,1024]{2,1,0:T(8,128)(2,1)}) custom-call(bf16[768,1280]{1,0:T(8,128)(2,1)} %all-gather.5.cloned.1.call-done.hid, bf16[768,1792]{1,0:T(8,128)(2,1)} %bitcast.80, bf16[2,2,768,1024]{3,2,1,0:T(8,128)(2,1)} %bitcast.76, ...), custom_call_target="tpu_custom_call", output_to_operand_aliasing={{0}: (5, {}), {1}: (6, {})} | custom-call | flops 4026531840 | bytes 7864320 | tf_op jit(solution)/shard_map/grads0_2/pallas_call | solution.py:615
  453.3 0.7 copy.30
  454.0 0.7 copy.31
  (30 shorter events, 1.0 us)
Async XLA Ops:
  7.2 361.0 %all-gather.3.cloned.1.call-start = ((), (), s32[]{:S(2)}) async-start(), calls=%async_computation | async-start | bytes 4423680 | tf_op jit(solution)/shard_map/all_gather | solution.py:646
  10.1 4.3 copy-start.11
  159.4 66.8 %copy-start.4 = (f32[192,1792]{1,0:T(8,128)S(1)}, f32[192,1792]{1,0:T(8,128)}, u32[]{:S(2)}) copy-start(f32[192,1792]{1,0:T(8,128)} %get-tuple-element.35) | copy-start | bytes 4128772
  228.8 64.6 %copy-start.5 = (f32[192,1792]{1,0:T(8,128)S(1)}, f32[192,1792]{1,0:T(8,128)}, u32[]{:S(2)}) copy-start(f32[192,1792]{1,0:T(8,128)} %get-tuple-element.36) | copy-start | bytes 4128772
  295.5 2.1 copy-start.2
  296.5 115.3 %all-gather.5.cloned.1.call-start = ((), (), s32[]{:S(2)}) async-start(), calls=%async_computation.1 | async-start | bytes 2457600 | tf_op jit(solution)/shard_map/all_gather | solution.py:646
  297.6 4.2 copy-start.3
  308.7 15.0 %copy-start.8 = (bf16[4,192,1792]{2,1,0:T(8,128)(2,1)S(1)}, bf16[4,192,1792]{2,1,0:T(8,128)(2,1)}, u32[]{:S(2)}) copy-start(bf16[4,192,1792]{2,1,0:T(8,128)(2,1)} %mul.88) | copy-start | bytes 8257540
  389.5 6.0 %copy-start = (bf16[768,2304]{1,0:T(8,128)(2,1)S(1)}, bf16[768,2304]{1,0:T(8,128)(2,1)}, u32[]{:S(2)}) copy-start(bf16[768,2304]{1,0:T(8,128)(2,1)} %all-gather.3.cloned.1.call-done.hid) | copy-start | bytes 10616836
  395.6 4.0 copy-start.9
  399.5 5.2 %copy-start.1 = (bf16[4,192,1792]{2,1,0:T(8,128)(2,1)S(1)}, bf16[4,192,1792]{2,1,0:T(8,128)(2,1)}, u32[]{:S(2)}) copy-start(bf16[4,192,1792]{2,1,0:T(8,128)(2,1)} %get-tuple-element.32.signs) | copy-start | bytes 8257540
  411.8 4.7 %copy-start.6 = (f32[768,1024]{1,0:T(8,128)S(1)}, f32[768,1024]{1,0:T(8,128)}, u32[]{:S(2)}) copy-start(f32[768,1024]{1,0:T(8,128)} %convolution_add_fusion) | copy-start | bytes 9437188
  411.8 4.7 %copy-start.7 = (f32[768,1024]{1,0:T(8,128)S(1)}, f32[768,1024]{1,0:T(8,128)}, u32[]{:S(2)}) copy-start(f32[768,1024]{1,0:T(8,128)} %convolution_add_fusion.1) | copy-start | bytes 9437188
  411.8 4.8 %copy-start.10 = (bf16[768,1280]{1,0:T(8,128)(2,1)S(1)}, bf16[768,1280]{1,0:T(8,128)(2,1)}, u32[]{:S(2)}) copy-start(bf16[768,1280]{1,0:T(8,128)(2,1)} %all-gather.5.cloned.1.call-done.hid) | copy-start | bytes 5898244
Sparse Core Ops, SparseCore 0:
  296.6 71.5 all-gather.2
  369.8 41.9 all-gather.4
